TPU v7x, 32 devices: a whole 2x2x4 slice. The times are simulated.
32 devices in a mesh: rep: 4 (over y, core), shard: 8 (over z, x).
Axes of the slice: x: 2, y: 2, z: 4, core: 2. Of those that a mesh axis runs over, the one named last changes fastest.
Arguments:
- hidden: bfloat16 [14336, 3584], P(('rep', 'shard')), may hold values from -144 to 144
- cotangent: bfloat16 [14336, 1024], P(('rep', 'shard')), may hold values from -6 to 6
- seq_ids: int32 [32, 448], P(('rep', 'shard')), may hold values from 0 to 3, as said below
- response_mask: int32 [32, 448], P(('rep', 'shard')), may hold values from 0 to 1, as said below
- group_ids: int32 [32, 4], P(('rep', 'shard')), may hold values from 0 to 15
- rewards: float32 [32, 4], P(('rep', 'shard')), may hold values from -6 to 6
- new_logp: float32 [32, 448], P(('rep', 'shard')), may hold values from -1.5 to -0.1
- old_logp: float32 [32, 448], P(('rep', 'shard')), may hold values from -1.5 to -0.1
- ref_logp: float32 [32, 448], P(('rep', 'shard')), may hold values from -1.5 to -0.1
- master: float32 [3, 3584, 1024], P(None, 'shard'), may hold values from -6 to 6
Outputs:
- new_master: float32 [3584, 1024], P('shard')
- rollout: bfloat16 [3, 3584, 2048], P(None, None, 'shard')
Inputs may be any that keep to these rules, and one draw needn't show every extreme that they name: `seq_ids`: each row numbers its device's 4 sequences in token order, never falling, each with one token or more. `response_mask`: within a sequence, prompt tokens come before response tokens; a sequence may have no response tokens.
All inputs are finite; a program needn't handle non-finite values.
Results may differ from a plain program's by a relative error of at most 0.0095.
Values may be sent and summed in bfloat16 or wider, within the bound.
A program may use at most 128 MiB of HBM per device.

v0:
```python
import functools

import jax
import jax.numpy as jnp
from jax import lax
from jax.experimental import pallas as pl
from jax.experimental.pallas import tpu as pltpu
from jax.sharding import PartitionSpec as P

HEAD = 128
KV_HEADS = 4
TP = 8
SEQ_DEV = 4
WIDE = 2 * HEAD
LANES = 128
SUB = 16
TILE = 256
MESH = pl.DeviceIdType.MESH


def token_rows(seq_row, mask_row, new_row, old_row, ref_row):
    maskf = mask_row.astype(jnp.float32)
    onehot = [(seq_row == j).astype(jnp.float32) for j in range(SEQ_DEV)]
    tok_len = jnp.zeros_like(maskf)
    for hot in onehot:
        tok_len = tok_len + hot * jnp.maximum(jnp.sum(maskf * hot, axis=1, keepdims=True), 1.0)
    weight = maskf / tok_len
    ratio = -weight * jnp.exp(new_row - old_row)
    return [hot * ratio for hot in onehot] + [weight * (0.2 * (1.0 - jnp.exp(ref_row - new_row)))]


def flip(index, bit):
    step = 1 << bit
    here = (index // step) % 2
    return index + (1 - 2 * here) * step, here


def exchange_kernel(
    n_rep, n_shard, split, group_ref, reward_ref, seq_ref, mask_ref, new_ref, old_ref, ref_ref,
    hidden_ref, cot_ref, master_ref,
    mb_ref, gb_out, nm_out, scale_ref,
    part, sums, zin, grad, rows_in, delta, stage_in, stage_out,
    small, small_in, token_t, send_sems, recv_sems, local_sems,
):
    z_count = n_shard // 2
    rep_bits = n_rep.bit_length() - 1
    dims = rep_bits
    r, s = lax.axis_index("rep"), lax.axis_index("shard")
    core, x, zi = r % 2, s % 2, s // 2
    head = zi % KV_HEADS
    first = zi - head
    features, toks = hidden_ref.shape[1], hidden_ref.shape[0]
    layer_count, rows = master_ref.shape[0], master_ref.shape[1]
    sub = rows // split
    counter = [0]
    started = []

    def send(src, dst, device):
        number = counter[0]
        counter[0] += 1
        copy = pltpu.make_async_remote_copy(
            src_ref=src, dst_ref=dst, send_sem=send_sems.at[number], recv_sem=recv_sems.at[number],
            device_id=device, device_id_type=MESH,
        )
        copy.start()
        started.append(copy)
        return copy

    def local(src, dst, number):
        copy = pltpu.make_async_copy(src, dst, local_sems.at[number])
        copy.start()
        return copy

    mate = (flip(r, 0)[0], s)
    options = []
    for bit in range(1, rep_bits):
        other, here = flip(r, bit)
        options.append((other, s, here))
    other, here = flip(s, 0)
    options.append((r, other, here))
    partners, bits = [], []
    for i in range(dims):
        a, b = options[i], options[(i + 1) % dims]
        partners.append(tuple(a[k] + core * (b[k] - a[k]) for k in range(2)))
        bits.append(a[2] + core * (b[2] - a[2]))
    z_peers = [None] + [(r, ((zi + d) % z_count) * 2 + x) for d in range(1, z_count)]
    tp_zi = [first + (head + d) % KV_HEADS for d in range(KV_HEADS)]
    tp_peers = [(r, tp_zi[d] * 2 + x) for d in range(KV_HEADS)]

    quarter = r % split
    fetch = local(master_ref.at[:, pl.ds(pl.multiple_of(quarter * sub, SUB), sub), :], stage_in, 0)

    barrier = pltpu.get_barrier_semaphore()
    everyone = n_rep * n_shard
    me = r * n_shard + s

    @pl.loop(1, everyone)
    def _(i):
        peer = (me + i) % everyone
        pl.semaphore_signal(
            barrier, inc=1, device_id=(peer // n_shard, peer % n_shard), device_id_type=MESH)

    shape = small.shape[1:]
    line = lax.broadcasted_iota(jnp.int32, shape, 0)
    lane = lax.broadcasted_iota(jnp.int32, shape, 1)
    hot, reward = jnp.zeros(shape, jnp.float32), jnp.zeros(shape, jnp.float32)
    for j in range(SEQ_DEV):
        hot = jnp.where((line == j) & (lane == group_ref[0, j]), 1.0, hot)
        reward = jnp.where(line == j, reward_ref[0, j], reward)
    small[0] = jnp.concatenate(
        [jnp.sum(hot, axis=0, keepdims=True), jnp.sum(hot * reward, axis=0, keepdims=True),
         jnp.sum(hot * (reward * reward), axis=0, keepdims=True),
         jnp.zeros((5, hot.shape[1]), jnp.float32)], axis=0)
    token_t[...] = jnp.zeros_like(token_t)
    terms = token_rows(seq_ref[...], mask_ref[...], new_ref[...], old_ref[...], ref_ref[...])
    for j, row in enumerate(terms):
        token_t[j:j + 1, :toks] = row
    tokens = jnp.transpose(token_t[...])[:toks]
    pl.semaphore_wait(barrier, everyone - 1)

    stat_copies = [send(small.at[0], small_in.at[d - 1], z_peers[d]) for d in range(1, z_count)]

    fetch.wait()
    for h in range(KV_HEADS):
        for l in range(layer_count):
            stage_out[h, l, :, :HEAD] = stage_in[l, :, h * HEAD:(h + 1) * HEAD].astype(jnp.bfloat16)
            low = KV_HEADS * HEAD + h * HEAD
            stage_out[h, l, :, HEAD:] = stage_in[l, :, low:low + HEAD].astype(jnp.bfloat16)
    yi = quarter // 2
    xy = [(r, flip(s, 0)[0])]
    first_at = (1 - x, yi)
    if split == 4:
        other = flip(r, 1)[0]
        xy = [(r + core * (other - r), s + (1 - core) * (1 - 2 * x)),
              (r + (1 - core) * (other - r), s + core * (1 - 2 * x))]
        first_at = (x + (1 - core) * (1 - 2 * x), yi + core * (1 - 2 * yi))
        second_at = (x + core * (1 - 2 * x), yi + (1 - core) * (1 - 2 * yi))
        third_at = (1 - x, 1 - yi)
    spread_copies = []

    def spread_block(d):
        for e in range(d, z_count if d == KV_HEADS - 1 else d + 1):
            if e:
                m1[e - 1].wait_recv()
            else:
                own_copy.wait()
            block = mb_ref.at[core, x, yi, (zi + z_count - e) % z_count]
            spread_copies.append([send(block, block, device) for device in xy])

    for copy in stat_copies:
        copy.wait_recv()
    slot = z_count - 1
    total = small[0]
    for d in range(1, z_count):
        total = total + small_in[d - 1]
    small[1] = total
    level = 1
    for k, device in enumerate([mate] + partners):
        copy = send(small.at[level], small_in.at[slot], device)
        if k == 0:
            own_copy = local(stage_out.at[head], mb_ref.at[core, x, yi, zi], 1)
            m1 = [send(stage_out.at[(head + d) % KV_HEADS], mb_ref.at[core, x, yi, zi], z_peers[d])
                  for d in range(1, z_count)]
        if k == 1:
            spread_block(0)
        copy.wait_recv()
        total = total + small_in[slot]
        slot += 1
        level += 1
        small[level] = total

    count = jnp.maximum(total[0:1], 1.0)
    mean = total[1:2] / count
    spread = jnp.maximum(jnp.sqrt(jnp.maximum(total[2:3] / count - mean * mean, 0.0)), 0.5)
    own_mean = jnp.sum(hot * mean, axis=1, keepdims=True)
    own_std = jnp.sum(hot * spread, axis=1, keepdims=True)
    own_std = jnp.where(own_std > 0.0, own_std, 1.0)
    advantage = (reward[:, 0:1] - own_mean) / own_std
    coef = tokens[:, SEQ_DEV:SEQ_DEV + 1]
    for j in range(SEQ_DEV):
        coef = coef + tokens[:, j:j + 1] * advantage[j:j + 1, :]
    for h in range(KV_HEADS):
        for side in range(2):
            low = side * KV_HEADS * HEAD + h * HEAD
            at = h * WIDE + side * HEAD
            delta[:, at:at + HEAD] = (coef * cot_ref[:, low:low + HEAD].astype(jnp.float32)).astype(jnp.bfloat16)

    spread_block(1)
    half = features // 2

    def multiply(base):
        @pl.loop(0, half // TILE)
        def _(i):
            at = pl.multiple_of(base + i * TILE, TILE)
            out = lax.dot_general(
                hidden_ref[:, pl.ds(at, TILE)], delta[...], (((0,), (0,)), ((), ())),
                preferred_element_type=jnp.float32,
            ).astype(jnp.bfloat16)
            for h in range(KV_HEADS):
                part[h, pl.ds(at, TILE), :] = out[:, h * WIDE:(h + 1) * WIDE]

    offsets, lens = [core * half], [half]
    for i in range(dims):
        lens.append(lens[-1] // 2)
        offsets.append(offsets[-1] + bits[i] * lens[-1])
    starts, at = [], 0
    for length in lens:
        starts.append(at)
        at += length
    order = [(head + k + 1) % KV_HEADS for k in range(KV_HEADS)]

    away = (1 - core) * half
    multiply(away)
    inbound = {}
    for k in range(KV_HEADS):
        inbound[0, k] = send(
            part.at[order[k], pl.ds(pl.multiple_of(away, SUB), half)],
            sums.at[order[k], pl.ds(starts[0], half)], mate)
    spread_block(2)
    multiply(core * half)

    spread_block(3)
    own_block = mb_ref.at[core, x, yi]
    to_mate = [send(own_block, own_block, mate)]
    forward = []

    inner = min(lens[-1], 112)

    def add_in(i, h):
        base = offsets[i]

        @pl.loop(0, lens[i] // inner)
        def _(t):
            at = pl.multiple_of(base + t * inner, SUB)
            from_at = pl.multiple_of(starts[i] + t * inner, SUB)
            part[h, pl.ds(at, inner), :] = (
                part[h, pl.ds(at, inner), :].astype(jnp.float32)
                + sums[h, pl.ds(from_at, inner), :].astype(jnp.float32)
            ).astype(jnp.bfloat16)

    z_copies = []
    for t in range(KV_HEADS + dims):
        for i in range(dims + 1):
            k = t - i
            if k < 0 or k >= KV_HEADS:
                continue
            inbound[i, k].wait_recv()
            add_in(i, order[k])
            if i < dims:
                gone = offsets[i] + (1 - bits[i]) * lens[i + 1]
                inbound[i + 1, k] = send(
                    part.at[order[k], pl.ds(pl.multiple_of(gone, SUB), lens[i + 1])],
                    sums.at[order[k], pl.ds(starts[i + 1], lens[i + 1])], partners[i])
            else:
                for d in range(1, z_count):
                    if d % KV_HEADS == (k + 1) % KV_HEADS:
                        z_copies.append(send(
                            part.at[order[k], pl.ds(pl.multiple_of(offsets[-1], SUB), lens[-1])],
                            zin.at[d - 1], z_peers[d]))
        if t == 3 and split == 4:
            for pair in spread_copies:
                pair[0].wait_recv()
            block = mb_ref.at[core, first_at[0], first_at[1]]
            forward.append(send(block, block, xy[1]))
            to_mate.append(send(block, block, mate))

    for copy in z_copies:
        copy.wait_recv()
    base = offsets[-1]

    def gather_sum(t, acc):
        at = pl.multiple_of(base + t * inner, SUB)
        g = part[head, pl.ds(at, inner), :].astype(jnp.float32)
        for d in range(1, z_count):
            g = g + zin[d - 1, pl.ds(pl.multiple_of(t * inner, SUB), inner), :].astype(jnp.float32)
        grad[pl.ds(at, inner), :] = g.astype(jnp.bfloat16)
        return acc + jnp.sum(g * g, axis=0, keepdims=True)

    squares = lax.fori_loop(0, lens[-1] // inner, gather_sum, jnp.zeros((1, WIDE), jnp.float32))
    square = jnp.broadcast_to(jnp.sum(squares, axis=1, keepdims=True), small.shape[1:])
    mine = pl.ds(pl.multiple_of(base, SUB), lens[-1])
    s_dst, inside = base // rows, base % rows
    pieces = rows // lens[-1]
    nm_number = counter[0]
    nm_in = nm_number + n_rep // 2
    counter[0] = nm_in + KV_HEADS * pieces
    nm_copies = [
        pltpu.make_async_remote_copy(
            src_ref=grad.at[mine], dst_ref=rows_in.at[head, pl.ds(pl.multiple_of(inside, SUB), lens[-1])],
            send_sem=send_sems.at[nm_number + j],
            recv_sem=recv_sems.at[nm_in + head * pieces + inside // lens[-1]],
            device_id=(2 * j + core, s_dst), device_id_type=MESH)
        for j in range(n_rep // 2)]
    dst_zi = s_dst // 2
    leaves = (dst_zi != zi) & (dst_zi // KV_HEADS == zi // KV_HEADS)
    level += 1
    small[level] = square
    square_copies = []
    for d in range(1, KV_HEADS):
        square_copies.append(send(small.at[level], small_in.at[slot], tp_peers[d]))
        slot += 1
    slot_base = slot - (KV_HEADS - 1)

    first_span = pl.ds(pl.multiple_of(offsets[dims], SUB), lens[dims])
    first_copy = send(grad.at[first_span], grad.at[first_span], partners[dims - 1])

    @pl.when(leaves)
    def _():
        for copy in nm_copies:
            copy.start()

    for step, i in enumerate(list(reversed(range(dims))) + [-1]):
        device = mate if i < 0 else partners[i]
        span = pl.ds(pl.multiple_of(offsets[i + 1], SUB), lens[i + 1])
        copy = first_copy if step == 0 else send(grad.at[span], grad.at[span], device)
        if step == 0:
            for other in square_copies:
                other.wait_recv()
            for d in range(KV_HEADS - 1):
                square = square + small_in[slot_base + d]
        level += 1
        small[level] = square
        square_copy = send(small.at[level], small_in.at[slot], device)
        square_copy.wait_recv()
        square = square + small_in[slot]
        slot += 1
        copy.wait_recv()

    if split == 4:
        for pair in spread_copies:
            pair[1].wait_recv()
        block = mb_ref.at[core, second_at[0], second_at[1]]
        to_mate.append(send(block, block, mate))
        forward[0].wait_recv()
        block = mb_ref.at[core, third_at[0], third_at[1]]
    else:
        for pair in spread_copies:
            pair[0].wait_recv()
        block = mb_ref.at[core, first_at[0], first_at[1]]
    to_mate.append(send(block, block, mate))

    rms = jnp.sqrt(square / (features * KV_HEADS * WIDE) + 1e-06)
    scale_ref[...] = 0.5 / rms[:, :LANES]
    done = [local(grad, gb_out, 0)]
    done.append(local(grad.at[pl.ds(pl.multiple_of(s * rows, SUB), rows)], nm_out.at[head], 1))
    others = [(head + d) % KV_HEADS for d in range(1, KV_HEADS)]
    pass_number = counter[0]
    counter[0] += KV_HEADS - 1
    passed = [
        pltpu.make_async_remote_copy(
            src_ref=rows_in.at[h], dst_ref=rows_in.at[h], send_sem=send_sems.at[pass_number + n],
            recv_sem=recv_sems.at[pass_number + n], device_id=mate, device_id_type=MESH)
        for n, h in enumerate(others)]
    keeper = (s * rows) // half

    @pl.when(core == keeper)
    def _():
        for n, h in enumerate(others):
            for p in range(pieces):
                pltpu.make_async_remote_copy(
                    src_ref=rows_in.at[h, pl.ds(p * lens[-1], lens[-1])],
                    dst_ref=rows_in.at[h, pl.ds(p * lens[-1], lens[-1])],
                    send_sem=send_sems.at[nm_number], recv_sem=recv_sems.at[nm_in + h * pieces + p],
                    device_id=mate, device_id_type=MESH).wait_recv()
            passed[n].start()

    @pl.when(core != keeper)
    def _():
        for copy in passed:
            copy.wait_recv()

    for n, h in enumerate(others):
        done.append(local(rows_in.at[h], nm_out.at[h], n + 2))
    for copy in to_mate:
        copy.wait_recv()

    @pl.when(core == keeper)
    def _():
        for copy in passed:
            copy.wait_send()

    @pl.when(leaves)
    def _():
        for copy in nm_copies:
            copy.wait_send()

    for copy in done:
        copy.wait()
    for copy in started:
        copy.wait_send()


def finish_kernel(mb_ref, gb_ref, nm_ref, scale_ref, master_ref, new_ref, out_ref):
    scale = scale_ref[0:1, 0:1]
    for h in range(KV_HEADS):
        for side in range(2):
            low = side * KV_HEADS * HEAD + h * HEAD
            new_ref[:, low:low + HEAD] = (
                master_ref[0, :, low:low + HEAD]
                - scale * nm_ref[h, :, side * HEAD:(side + 1) * HEAD].astype(jnp.float32))
    _, _, y_count, z_count, layer_count, sub, _ = mb_ref.shape
    for z in range(z_count):
        for x in range(2):
            for y in range(y_count):
                for c in range(2):
                    at = (((z * 2 + x) * y_count + y) * 2 + c) * sub
                    span = slice(at, at + sub)
                    out_ref[0, span, :] = (
                        mb_ref[c, x, y, z, 0].astype(jnp.float32)
                        - scale * gb_ref[span, :].astype(jnp.float32)).astype(jnp.bfloat16)
                    for l in range(1, layer_count):
                        out_ref[l, span, :] = mb_ref[c, x, y, z, l]


def per_device(
    n_rep, n_shard, hidden, cotangent, seq_ids, response_mask, group_ids, rewards, new_logp, old_logp, ref_logp,
    master,
):
    groups = n_rep * n_shard * SEQ_DEV // 8
    wide = -(-groups // LANES) * LANES
    toks, features = hidden.shape
    layer_count, rows, cols = master.shape
    z_count = n_shard // 2
    split = 4 if n_rep % 4 == 0 and (rows // 4) % SUB == 0 else 2
    sub = rows // split
    dims = n_rep.bit_length() - 1
    final = features // 2 ** (dims + 1)
    bf16, f32 = jnp.bfloat16, jnp.float32
    vmem, hbm = pl.BlockSpec(memory_space=pltpu.VMEM), pl.BlockSpec(memory_space=pl.ANY)
    smem = pl.BlockSpec(memory_space=pltpu.SMEM)
    mb_shape = (2, 2, split // 2, z_count, layer_count, sub, WIDE)
    sem_count = 64 + 8 * z_count
    landing = features // 2 * 2
    mb, gb, nm, scale = pl.pallas_call(
        functools.partial(exchange_kernel, n_rep, n_shard, split),
        out_shape=(
            jax.ShapeDtypeStruct(mb_shape, bf16),
            jax.ShapeDtypeStruct((features, WIDE), bf16),
            jax.ShapeDtypeStruct((KV_HEADS, rows, WIDE), bf16),
            jax.ShapeDtypeStruct((8, LANES), f32),
        ),
        in_specs=[smem] * 2 + [vmem] * 7 + [hbm],
        out_specs=(hbm, hbm, hbm, vmem),
        scratch_shapes=[
            pltpu.VMEM((KV_HEADS, features, WIDE), bf16),
            pltpu.VMEM((KV_HEADS, landing, WIDE), bf16),
            pltpu.VMEM((z_count - 1, final, WIDE), bf16),
            pltpu.VMEM((features, WIDE), bf16),
            pltpu.VMEM((KV_HEADS, rows, WIDE), bf16),
            pltpu.VMEM((toks, cols), bf16),
            pltpu.VMEM((layer_count, sub, cols), f32),
            pltpu.VMEM((KV_HEADS, layer_count, sub, WIDE), bf16),
            pltpu.VMEM((2 * dims + 6, 8, wide), f32),
            pltpu.VMEM((z_count + 2 * dims + 6, 8, wide), f32),
            pltpu.VMEM((LANES, -(-toks // LANES) * LANES), f32),
            pltpu.SemaphoreType.DMA((sem_count,)),
            pltpu.SemaphoreType.DMA((sem_count,)),
            pltpu.SemaphoreType.DMA((8,)),
        ],
        compiler_params=pltpu.CompilerParams(
            collective_id=0, has_side_effects=True, vmem_limit_bytes=56 * 2**20
        ),
        name="exchange",
    )(group_ids, rewards, seq_ids, response_mask, new_logp, old_logp, ref_logp, hidden, cotangent, master)
    steps = KV_HEADS
    new_master, rollout = pl.pallas_call(
        finish_kernel,
        grid=(steps,),
        out_shape=(
            jax.ShapeDtypeStruct((rows, cols), f32),
            jax.ShapeDtypeStruct((layer_count, features, WIDE), bf16),
        ),
        in_specs=[
            pl.BlockSpec((2, 2, split // 2, z_count // steps, layer_count, sub, WIDE),
                         lambda i: (0, 0, 0, i, 0, 0, 0)),
            pl.BlockSpec((features // steps, WIDE), lambda i: (i, 0)),
            pl.BlockSpec((KV_HEADS, rows // steps, WIDE), lambda i: (0, i, 0)),
            pl.BlockSpec((8, LANES), lambda i: (0, 0)),
            pl.BlockSpec((1, rows // steps, cols), lambda i: (0, i, 0)),
        ],
        out_specs=(
            pl.BlockSpec((rows // steps, cols), lambda i: (i, 0)),
            pl.BlockSpec((layer_count, features // steps, WIDE), lambda i: (0, i, 0)),
        ),
        name="finish",
    )(mb, gb, nm, scale, master)
    return (new_master, rollout)


def solution(mesh):
    tokens = P(("rep", "shard"), None)
    return jax.shard_map(
        functools.partial(per_device, mesh.shape["rep"], mesh.shape["shard"]),
        mesh=mesh,
        in_specs=(tokens,) * 9 + (P(None, "shard", None),),
        out_specs=(P("shard", None), P(None, None, "shard")),
        check_vma=False,
    )
```

profile of v0, /device:TPU:0, one launch (start us, length us, event | category | flops | bytes accessed | tf_op | source)
XLA Modules:
  0.0 117.3 jit_solution(13009146937844125613)
XLA Ops:
  0.6 109.8 %exchange.1 = (bf16[2,2,2,4,3,112,256]{6,5,4,3,2,1,0:T(8,128)(2,1)}, bf16[3584,256]{1,0:T(8,128)(2,1)}, bf16[4,448,256]{2,1,0:T(8,128)(2,1)}, f32[8,128]{1,0:T(8,128)}) custom-call(s32[1,4]{1,0:T(1,128)} %group_ref.1, f32[1,4]{1,0:T(1,128)} %reward_ref.1, s32[1,448]{1,0:T(1,128)} %seq_ref.1, s32[1,448]{1,0:T(1,128)} %mask_ref.1, f32[1,448]{1,0:T(1,128)} %new_ref.1, ...), custom_call_target="tpu_custom_call" | custom-call | tf_op jit(solution)/shard_map/exchange/pallas_call | solution.py:434
  110.4 6.9 %finish.1 = (f32[448,1024]{1,0:T(8,128)}, bf16[3,3584,256]{2,1,0:T(8,128)(2,1)}) custom-call(bf16[2,2,2,4,3,112,256]{6,5,4,3,2,1,0:T(8,128)(2,1)} %get-tuple-element.6.mb_ref, bf16[3584,256]{1,0:T(8,128)(2,1)} %get-tuple-element.7.gb_ref, bf16[4,448,256]{2,1,0:T(8,128)(2,1)} %get-tuple-element.8.nm_ref, f32[8,128]{1,0:T(8,128)} %get-tuple-element.9.scale_ref, ...), custom_call_target="tpu_custom_call" | custom-call | tf_op jit(solution)/shard_map/finish/pallas_call | solution.py:466
where the time goes:
time: 118 us; the launch traced here: 117 us
  Pallas kernels  117 us (99%)
    pallas_call x1, Pallas kernels, per_device(): pl.pallas_call(functools.partial(exchange_kernel, n_rep, n_shard, split),...  110 us
    pallas_call x1, Pallas kernels, per_device(): pl.pallas_call(finish_kernel, grid=(steps,), out_shape=(jax.ShapeDtypeStr...  6.91 us

commit v1 on v0

v1 whole, which is shorter than its diff:
```python
import functools

import jax
import jax.numpy as jnp
from jax import lax
from jax.experimental import pallas as pl
from jax.experimental.pallas import tpu as pltpu
from jax.sharding import PartitionSpec as P

HEAD = 128
KV_HEADS = 4
SEQ_DEV = 4
WIDE = 2 * HEAD
LANES = 128
SUB = 16
MESH = pl.DeviceIdType.MESH


def token_rows(seq_row, mask_row, new_row, old_row, ref_row):
    maskf = mask_row.astype(jnp.float32)
    onehot = [(seq_row == j).astype(jnp.float32) for j in range(SEQ_DEV)]
    tok_len = jnp.zeros_like(maskf)
    for hot in onehot:
        tok_len = tok_len + hot * jnp.maximum(jnp.sum(maskf * hot, axis=1, keepdims=True), 1.0)
    weight = maskf / tok_len
    ratio = -weight * jnp.exp(new_row - old_row)
    return [hot * ratio for hot in onehot] + [weight * (0.2 * (1.0 - jnp.exp(ref_row - new_row)))]


def flip(index, bit):
    step = 1 << bit
    here = (index // step) % 2
    return index + (1 - 2 * here) * step, here


def step_kernel(
    n_rep, n_shard, split, groups, group_hbm, reward_hbm, *args,
):
    token_hbm, args = args[:5], args[5:]
    step_body(n_rep, n_shard, split, groups, group_hbm, reward_hbm, token_hbm, *args)


def step_body(
    n_rep, n_shard, split, groups, group_hbm, reward_hbm, token_hbm,
    hidden_ref, cot_ref, master_ref,
    nm_ref, roll_ref,
    group_ref, reward_ref, ids_in, logp_in, small, stat_in, square_in, info_in, info_own, token_own, token_in, hid, hid_t, cot, delta, part, sums, zin,
    grad, grad_b, base_out, base_in, m0, stage_in, stage_out, rows_in,
    send_sems, recv_sems, local_sems, all_sems, set_send, set_recv,
):
    z_count = n_shard // 2
    dims = n_rep.bit_length() - 1
    everyone = n_rep * n_shard
    r, s = lax.axis_index("rep"), lax.axis_index("shard")
    me = r * n_shard + s
    core, y, x, zi = r % 2, r // 2, s % 2, s // 2
    head = zi % KV_HEADS
    toks, features = hidden_ref.shape
    half = features // 2
    layer_count, rows, cols = master_ref.shape
    sub = rows // split
    final = half // n_rep
    pieces = rows // final
    half_z = z_count // 2
    counter = [0]
    started = []

    def numbered():
        number = counter[0]
        counter[0] += 1
        return number

    def remote(src, dst, device, number, landing=None):
        return pltpu.make_async_remote_copy(
            src_ref=src, dst_ref=dst, send_sem=send_sems.at[number],
            recv_sem=recv_sems.at[number if landing is None else landing],
            device_id=device, device_id_type=MESH)

    def send(src, dst, device):
        copy = remote(src, dst, device, numbered())
        copy.start()
        started.append(copy)
        return copy

    def put(src, dst, device, gone, landed):
        pltpu.make_async_remote_copy(
            src_ref=src, dst_ref=dst, send_sem=set_send.at[gone], recv_sem=set_recv.at[landed],
            device_id=device, device_id_type=MESH).start()

    def whole(ref, number):
        return pltpu.make_async_remote_copy(
            src_ref=ref, dst_ref=ref, send_sem=set_send.at[number], recv_sem=set_recv.at[number],
            device_id=(flip(r, 0)[0], s), device_id_type=MESH)

    def local(src, dst, number):
        copy = pltpu.make_async_copy(src, dst, local_sems.at[number])
        copy.start()
        return copy

    def span(at, size):
        return pl.ds(pl.multiple_of(at, SUB), size)

    def to_all(src, dst, sem):
        @pl.loop(1, everyone)
        def _(i):
            peer = (me + i) % everyone
            pltpu.make_async_remote_copy(
                src_ref=src, dst_ref=dst.at[i - 1], send_sem=all_sems.at[sem], recv_sem=all_sems.at[sem + 1],
                device_id=(peer // n_shard, peer % n_shard), device_id_type=MESH).start()

        return pltpu.make_async_remote_copy(
            src_ref=dst, dst_ref=dst, send_sem=all_sems.at[sem], recv_sem=all_sems.at[sem + 1],
            device_id=(flip(r, 0)[0], s), device_id_type=MESH)

    mate = (flip(r, 0)[0], s)
    options = []
    for bit in range(1, dims):
        other, here = flip(r, bit)
        options.append((other, s, here))
    other, here = flip(s, 0)
    options.append((r, other, here))
    partners, bits = [], []
    for i in range(dims):
        a, b = options[i], options[(i + 1) % dims]
        partners.append(tuple(a[k] + core * (b[k] - a[k]) for k in range(2)))
        bits.append(a[2] + core * (b[2] - a[2]))
    z_peers = [None] + [(r, ((zi + d) % z_count) * 2 + x) for d in range(1, z_count)]

    def home(yy):
        low = yy // pieces
        return low + core * (z_count - 1 - 2 * low), yy % pieces

    def row_of(yy, xx):
        z, piece = home(yy)
        return (2 * z + xx) * rows + piece * final

    def across(yy, xx, i):
        moved = []
        for option in (i % dims, (i + 1) % dims):
            moved.append((flip(yy, option)[0], xx) if option < dims - 1 else (yy, 1 - xx))
        (ya, xa), (yb, xb) = moved
        return ya + core * (yb - ya), xa + core * (xb - xa)

    def spot(j, c):
        low, xx, piece = j // pieces // 2, j // pieces % 2, j % pieces
        yy = (low if c == 0 else half_z - 1 - low) * pieces + piece
        chosen = [(yy >> o) & 1 for o in range(dims - 1)] + [xx]
        return sum(chosen[(i + c) % dims] << (dims - 1 - i) for i in range(dims))

    home_z, home_piece = home(y)
    quarter = r % split
    own_half = pl.ds(pl.multiple_of(core * half, LANES), half)
    other_half = pl.ds(pl.multiple_of((1 - core) * half, LANES), half)
    fetch_stage = local(master_ref.at[pl.ds(1, layer_count - 1), span(quarter * sub, sub), :], stage_in, 0)
    fetch_hid = local(hidden_ref.at[:, own_half], hid.at[pl.ds(0, toks)], 1)
    fetch_cot = local(cot_ref, cot.at[0], 2)
    fetch_m0 = local(master_ref.at[0], m0, 3)
    fetch_small = [local(group_hbm, group_ref, 4), local(reward_hbm, reward_ref, 5)]
    fetch_tokens = [local(ref, ids_in.at[pl.ds(n, 1)], 6 + n) for n, ref in enumerate(token_hbm[:2])]
    fetch_tokens += [local(ref, logp_in.at[pl.ds(n, 1)], 8 + n) for n, ref in enumerate(token_hbm[2:])]

    barrier = pltpu.get_barrier_semaphore()

    @pl.loop(1, everyone)
    def _(i):
        peer = (me + i) % everyone
        pl.semaphore_signal(
            barrier, inc=1, device_id=(peer // n_shard, peer % n_shard), device_id_type=MESH)

    shape = info_in.shape
    line = lax.broadcasted_iota(jnp.int32, shape, 0)
    lane = lax.broadcasted_iota(jnp.int32, shape, 1)
    row_lane = lax.broadcasted_iota(jnp.int32, (1, shape[1]), 1)
    info = jnp.zeros(shape, jnp.float32)
    own_sums = jnp.zeros((1, shape[1]), jnp.float32)
    for copy in fetch_small:
        copy.wait()
    for j in range(SEQ_DEV):
        group, given = group_ref[0, j], reward_ref[0, j]
        info = jnp.where((line == j) & (lane == group), 1.0, info)
        info = jnp.where(line == SEQ_DEV + j, given, info)
        for n, value in enumerate((1.0, given, given * given)):
            own_sums = own_sums + jnp.where(row_lane == n * groups + group, value, 0.0)
    info_own[...] = info
    small[0] = own_sums
    token_own[...] = jnp.zeros_like(token_own)
    with jax.named_scope('w_barrier'):
        pl.semaphore_wait(barrier, everyone - 1)

    stats = to_all(small.at[0], stat_in, 0)
    mate_info = send(info_own, info_in, mate)
    mate_hid = send(hidden_ref.at[:, other_half], hid.at[pl.ds(toks, toks)], mate)
    mate_cot = send(cot_ref, cot.at[1], mate)

    with jax.named_scope('w_stage'):
        fetch_stage.wait()
    for h in range(KV_HEADS):
        low = KV_HEADS * HEAD + h * HEAD
        for l in range(layer_count - 1):
            stage_out[h, l, :, :HEAD] = stage_in[l, :, h * HEAD:(h + 1) * HEAD].astype(jnp.bfloat16)
            stage_out[h, l, :, HEAD:] = stage_in[l, :, low:low + HEAD].astype(jnp.bfloat16)

    def block(z, xx, yy):
        return roll_ref.at[pl.ds(1, layer_count - 1), span((2 * z + xx) * rows + (2 * yy + core) * sub, sub), :]

    yi = quarter // 2
    xy = [(r, flip(s, 0)[0])]
    first_at = (1 - x, yi)
    if split == 4:
        other = flip(r, 1)[0]
        xy = [(r + core * (other - r), s + (1 - core) * (1 - 2 * x)),
              (r + (1 - core) * (other - r), s + core * (1 - 2 * x))]
        first_at = (x + (1 - core) * (1 - 2 * x), yi + core * (1 - 2 * yi))
        second_at = (x + core * (1 - 2 * x), yi + (1 - core) * (1 - 2 * yi))
        third_at = (1 - x, 1 - yi)

    near = [zi]
    for e in range(1, z_count):
        z = zi
        for bit in range(z_count.bit_length() - 1):
            if e >> bit & 1:
                z = flip(z, bit)[0]
        near.append(z)
    m1 = [remote(stage_out.at[near[e] % KV_HEADS], block(zi, x, yi), (r, near[e] * 2 + x), numbered())
          for e in range(1, z_count)]
    for copy in m1:
        copy.start()
        started.append(copy)
    roll_ref[1:, span((2 * zi + x) * rows + quarter * sub, sub), :] = stage_out[head]
    SPREAD_0, SPREAD_1, FORWARD, TO_MATE, GATHER, PIECES, HALVES, GRADS, BASE = range(9)
    level_in = 9

    def spread_block(e):
        if e:
            with jax.named_scope(f'w_m1#{e}'):
                m1[e - 1].wait_recv()
        here = block(near[e], x, yi)
        for n, device in enumerate(xy):
            put(here, here, device, SPREAD_0 + n, SPREAD_0 + n)
        put(here, here, mate, TO_MATE, TO_MATE)

    spread_block(0)

    for copy in fetch_tokens:
        copy.wait()
    terms = token_rows(ids_in[0:1], ids_in[1:2], logp_in[0:1], logp_in[1:2], logp_in[2:3])
    for j, row in enumerate(terms):
        token_own[j:j + 1, :toks] = row
    mate_tok = send(token_own, token_in, mate)

    is_home = home_z == zi
    fetch_m0.wait()

    @pl.when(is_home)
    def _():
        at = span(home_piece * final, final)
        for h in range(KV_HEADS):
            low = KV_HEADS * HEAD + h * HEAD
            base_out[h, :, :HEAD] = m0[at, h * HEAD:(h + 1) * HEAD].astype(jnp.bfloat16)
            base_out[h, :, HEAD:] = m0[at, low:low + HEAD].astype(jnp.bfloat16)
        for d in range(1, z_count):
            put(base_out.at[(head + d) % KV_HEADS], base_in, z_peers[d], BASE, BASE)
        base_in[...] = base_out[head]

    with jax.named_scope('w_hid'):
        fetch_hid.wait()
        mate_hid.wait_recv()

    @pl.loop(0, half // WIDE)
    def _(t):
        at = pl.multiple_of(t * WIDE, WIDE)
        hid_t[pl.ds(at, WIDE), :] = jnp.transpose(hid[:, pl.ds(at, WIDE)])

    with jax.named_scope('w_cot'):
     fetch_cot.wait()
    mate_cot.wait_recv()
    mate_info.wait_recv()
    mate_tok.wait_recv()
    padded = token_own.shape[1]
    tokens = jnp.transpose(jnp.concatenate(
        [token_own[...], token_in[...], jnp.zeros((LANES - 16, padded), jnp.float32)], axis=0))[:toks]

    with jax.named_scope('w_stats'):
        stats.wait_recv()
    total = own_sums + jnp.sum(stat_in[...], axis=0)
    wide = shape[1]
    count = jnp.maximum(total, 1.0)
    mean = pltpu.roll(total, wide - groups, 1) / count
    spread_of = jnp.maximum(
        jnp.sqrt(jnp.maximum(pltpu.roll(total, wide - 2 * groups, 1) / count - mean * mean, 0.0)), 0.5)

    def coef_of(told, low):
        hots, given = told[:SEQ_DEV], told[SEQ_DEV:, 0:1]
        advantage = (given - jnp.sum(hots * mean, axis=1, keepdims=True)) / jnp.sum(
            hots * spread_of, axis=1, keepdims=True)
        out = tokens[:, low + SEQ_DEV:low + SEQ_DEV + 1]
        for j in range(SEQ_DEV):
            out = out + tokens[:, low + j:low + j + 1] * advantage[j:j + 1, :]
        return out

    coefs = [coef_of(info, 0), coef_of(info_in[...], 8)]

    lens, offsets = [half], [0]
    for i in range(dims):
        lens.append(lens[-1] // 2)
        offsets.append(offsets[-1] + bits[i] * lens[-1])
    starts, at = [], 0
    for length in lens[1:]:
        starts.append(at)
        at += length
    turns = [2, 1, 3, 0]
    order = [(head + d) % KV_HEADS for d in turns]
    tile = half // 2
    inbound = {(i, k): numbered() for i in range(dims) for k in range(KV_HEADS)}

    def halves(i, k):
        gone = offsets[i] + (1 - bits[i]) * lens[i + 1]
        return pltpu.make_async_remote_copy(
            src_ref=part.at[order[k], span(gone, lens[i + 1])],
            dst_ref=sums.at[order[k], pl.ds(starts[i], lens[i + 1])],
            send_sem=set_send.at[HALVES], recv_sem=recv_sems.at[inbound[i, k]],
            device_id=partners[i], device_id_type=MESH)

    def pass_on(i, k):
        halves(i, k).start()

    for k in range(KV_HEADS):
        h = order[k]
        for side in range(2):
            low = pl.ds(pl.multiple_of(side * KV_HEADS * HEAD + h * HEAD, HEAD), HEAD)
            for src in range(2):
                delta[src * toks:(src + 1) * toks, side * HEAD:(side + 1) * HEAD] = (
                    coefs[src] * cot[src, :, low].astype(jnp.float32)).astype(jnp.bfloat16)
        for t in range(2):
          with jax.named_scope(f'mul#k={k}'):
            out = jnp.dot(
                hid_t[t * tile:(t + 1) * tile, :], delta[...], preferred_element_type=jnp.float32
            ).astype(jnp.bfloat16)
            for q in range(tile // final):
                j = t * (tile // final) + q
                place = spot(j, 0) + core * (spot(j, 1) - spot(j, 0))
                part[h, span(place * final, final), :] = out[q * final:(q + 1) * final]
        pass_on(0, k)
        if k + 1 < KV_HEADS:
            spread_block(k + 1)
    for e in range(KV_HEADS, z_count):
        spread_block(e)

    inner = min(final, 112)

    def add_in(i, h):
        @pl.loop(0, lens[i + 1] // inner)
        def _(t):
            at = span(offsets[i + 1] + t * inner, inner)
            part[h, at, :] = (
                part[h, at, :].astype(jnp.float32)
                + sums[h, span(starts[i] + t * inner, inner), :].astype(jnp.float32)
            ).astype(jnp.bfloat16)

    last = dims - 1
    mine = span(offsets[dims], final)

    def z_send(k):
        for d in range(1, z_count):
            if d % KV_HEADS == turns[k]:
                put(part.at[order[k], mine], zin.at[d - 1], z_peers[d], GRADS, GRADS)

    for t in range(KV_HEADS + last):
        for i in range(dims):
            k = t - i
            if k < 0 or k >= KV_HEADS:
                continue
            with jax.named_scope(f'w_in#i={i}#k={k}'):
                halves(i, k).wait_recv()
            if i == last and k == KV_HEADS - 1 and z_count == KV_HEADS:
                continue
            add_in(i, order[k])
            if i < last:
                pass_on(i + 1, k)
            else:
                z_send(k)
    with jax.named_scope('w_z'):
        whole(zin, GRADS).wait_recv()

    def gather_sum(t, acc):
        g = part[head, span(offsets[dims] + t * inner, inner), :].astype(jnp.float32)
        if z_count == KV_HEADS:
            g = g + sums[head, span(starts[last] + t * inner, inner), :].astype(jnp.float32)
        at = span(t * inner, inner)
        for d in range(1, z_count):
            g = g + zin[d - 1, at, :].astype(jnp.float32)
        grad[at, :] = g
        grad_b[at, :] = g.astype(jnp.bfloat16)
        return acc + jnp.sum(g * g, axis=0, keepdims=True)

    squares = lax.fori_loop(0, final // inner, gather_sum, jnp.zeros((1, WIDE), jnp.float32))
    own_square = jnp.broadcast_to(jnp.sum(squares, axis=1, keepdims=True), (1, LANES))
    small[1, :, :LANES] = own_square
    all_squares = to_all(small.at[1, :, pl.ds(0, LANES)], square_in, 2)

    nm_numbers = [numbered() for _ in range(n_rep // 2)]
    nm_in = counter[0]
    counter[0] += KV_HEADS * pieces
    nm_copies = []
    for j in range(n_rep // 2):
        copy = remote(
            grad_b, rows_in.at[head, span(home_piece * final, final)], (2 * j + core, 2 * home_z + x),
            nm_numbers[j], nm_in + head * pieces + home_piece)
        leaves = (home_z // KV_HEADS == zi // KV_HEADS) & ((home_z != zi) | (j != y))
        nm_copies.append((leaves, copy))
        pl.when(leaves)(copy.start)

    @pl.when(is_home)
    def _():
        rows_in[head, span(home_piece * final, final), :] = grad_b[...]

    blocks = roll_ref.at[pl.ds(1, layer_count - 1), pl.ds(0, z_count * sub), :]
    with jax.named_scope('w_sp0'):
        whole(blocks, SPREAD_0).wait_recv()
    for z in near:
        got = block(z, *first_at)
        if split == 4:
            put(got, got, xy[1], FORWARD, FORWARD)
        put(got, got, mate, TO_MATE, TO_MATE)

    @pl.when(home_z != zi)
    def _():
        whole(base_in, BASE).wait_recv()

    with jax.named_scope('w_squares'):
        all_squares.wait_recv()
    square = own_square + jnp.sum(square_in[...], axis=0)
    rms = jnp.sqrt(square[:, 0:1] / (features * KV_HEADS * WIDE) + 1e-06)
    scale = 0.5 / rms
    row_me = row_of(y, x)

    @pl.loop(0, final // inner)
    def _(t):
        at = span(t * inner, inner)
        roll_ref[0, span(row_me + t * inner, inner), :] = (
            base_in[at, :].astype(jnp.float32) - scale * grad[at, :]).astype(jnp.bfloat16)

    def layer0(yy, xx):
        return roll_ref.at[0, span(row_of(yy, xx), final), :]

    def gather_in(i):
        return whole(roll_ref.at[0, pl.ds(0, final << (dims - 1 - i)), :], level_in + i)

    have, passed = [(y, x)], 0
    for i in reversed(range(dims)):
        for at in have:
            put(layer0(*at), layer0(*at), partners[i], GATHER, level_in + i)
        for at in have[passed:]:
            put(layer0(*at), layer0(*at), mate, PIECES, PIECES)
        passed = len(have)
        have = have + [across(*at, i) for at in have]
        if i:
            with jax.named_scope(f'w_ag#{i}'):
                gather_in(i).wait_recv()

    keeper = zi // half_z
    pass_number = [numbered() for _ in range(KV_HEADS)]
    hand_over = [remote(rows_in.at[h], rows_in.at[h], mate, pass_number[h]) for h in range(KV_HEADS)]

    def landed(h, p):
        return remote(
            rows_in.at[h, pl.ds(p * final, final)], rows_in.at[h, pl.ds(p * final, final)], mate,
            nm_numbers[0], nm_in + h * pieces + p)

    @pl.when(core == keeper)
    @jax.named_scope('w_rows')
    def _():
        low = zi + core * (z_count - 1 - 2 * zi)
        for h in range(KV_HEADS):
            for p in range(pieces):
                @pl.when((h != head) | (y != low * pieces + p))
                def _():
                    landed(h, p).wait_recv()
            hand_over[h].start()

    if split == 4:
        with jax.named_scope('w_sp1'):
            whole(blocks, SPREAD_1).wait_recv()
        with jax.named_scope('w_fwd'):
            whole(blocks, FORWARD).wait_recv()
        for z in near:
            for there in (second_at, third_at):
                got = block(z, *there)
                put(got, got, mate, TO_MATE, TO_MATE)
    with jax.named_scope('w_gathered'):
        gather_in(0).wait_recv()
    for at in have[passed:]:
        put(layer0(*at), layer0(*at), mate, PIECES, PIECES)

    @pl.when(core != keeper)
    @jax.named_scope('w_hand')
    def _():
        for copy in hand_over:
            copy.wait_recv()

    for h in range(KV_HEADS):
        for side in range(2):
            low = side * KV_HEADS * HEAD + h * HEAD
            nm_ref[:, low:low + HEAD] = (
                m0[:, low:low + HEAD] - scale * rows_in[h, :, side * HEAD:(side + 1) * HEAD].astype(jnp.float32))

    all_blocks = roll_ref.at[pl.ds(1, layer_count - 1), pl.ds(0, z_count * split * sub), :]
    all_pieces = roll_ref.at[0, pl.ds(0, n_rep * final), :]
    with jax.named_scope('w_mate'):
        whole(all_blocks, TO_MATE).wait_recv()
        whole(all_pieces, PIECES).wait_recv()

    @pl.when(core == keeper)
    def _():
        for copy in hand_over:
            copy.wait_send()

    @pl.when(is_home)
    def _():
        whole(zin, BASE).wait_send()

    for leaves, copy in nm_copies:
        pl.when(leaves)(copy.wait_send)
    for copy in started:
        copy.wait_send()
    whole(blocks, SPREAD_0).wait_send()
    if split == 4:
        whole(blocks, SPREAD_1).wait_send()
        whole(blocks, FORWARD).wait_send()
    whole(all_blocks, TO_MATE).wait_send()
    whole(all_pieces, PIECES).wait_send()
    whole(roll_ref.at[0, pl.ds(0, (n_rep - 1) * final), :], GATHER).wait_send()
    whole(part.at[:, pl.ds(0, half - final), :], HALVES).wait_send()
    whole(zin, GRADS).wait_send()
    stats.wait_send()
    all_squares.wait_send()


def per_device(
    n_rep, n_shard, hidden, cotangent, seq_ids, response_mask, group_ids, rewards, new_logp, old_logp, ref_logp,
    master,
):
    everyone = n_rep * n_shard
    groups = everyone * SEQ_DEV // 8
    wide = -(-3 * groups // LANES) * LANES
    toks, features = hidden.shape
    layer_count, rows, cols = master.shape
    z_count = n_shard // 2
    split = 4 if n_rep % 4 == 0 and (rows // 4) % SUB == 0 else 2
    sub = rows // split
    half = features // 2
    final = half // n_rep
    pad = -(-toks // LANES) * LANES
    bf16, f32 = jnp.bfloat16, jnp.float32
    vmem, hbm = pl.BlockSpec(memory_space=pltpu.VMEM), pl.BlockSpec(memory_space=pltpu.HBM)
    sem_count = 96 + 12 * z_count + 6 * n_rep
    return pl.pallas_call(
        functools.partial(step_kernel, n_rep, n_shard, split, groups),
        out_shape=(pltpu.VMEM((rows, cols), f32), pltpu.VMEM((layer_count, features, WIDE), bf16)),
        in_specs=[hbm] * 10,
        out_specs=(vmem, vmem),
        scratch_shapes=[
            pltpu.SMEM((1, SEQ_DEV), jnp.int32),
            pltpu.SMEM((1, SEQ_DEV), f32),
            pltpu.VMEM((2, toks), jnp.int32),
            pltpu.VMEM((3, toks), f32),
            pltpu.VMEM((2, 1, wide), f32),
            pltpu.VMEM((everyone - 1, 1, wide), f32),
            pltpu.VMEM((everyone - 1, 1, LANES), f32),
            pltpu.VMEM((8, wide), f32),
            pltpu.VMEM((8, wide), f32),
            pltpu.VMEM((8, pad), f32),
            pltpu.VMEM((8, pad), f32),
            pltpu.VMEM((2 * toks, half), bf16),
            pltpu.VMEM((half, 2 * toks), bf16),
            pltpu.VMEM((2, toks, cols), bf16),
            pltpu.VMEM((2 * toks, WIDE), bf16),
            pltpu.VMEM((KV_HEADS, half, WIDE), bf16),
            pltpu.VMEM((KV_HEADS, half, WIDE), bf16),
            pltpu.VMEM((z_count - 1, final, WIDE), bf16),
            pltpu.VMEM((final, WIDE), f32),
            pltpu.VMEM((final, WIDE), bf16),
            pltpu.VMEM((KV_HEADS, final, WIDE), bf16),
            pltpu.VMEM((final, WIDE), bf16),
            pltpu.VMEM((rows, cols), f32),
            pltpu.VMEM((layer_count - 1, sub, cols), f32),
            pltpu.VMEM((KV_HEADS, layer_count - 1, sub, WIDE), bf16),
            pltpu.VMEM((KV_HEADS, rows, WIDE), bf16),
            pltpu.SemaphoreType.DMA((sem_count,)),
            pltpu.SemaphoreType.DMA((sem_count,)),
            pltpu.SemaphoreType.DMA((12,)),
            pltpu.SemaphoreType.DMA((4,)),
            pltpu.SemaphoreType.DMA((12 + n_rep,)),
            pltpu.SemaphoreType.DMA((12 + n_rep,)),
        ],
        compiler_params=pltpu.CompilerParams(
            collective_id=0, has_side_effects=True, vmem_limit_bytes=44 * 2**20
        ),
        name="step",
    )(*(pltpu.with_memory_space_constraint(value, pltpu.HBM) for value in (
        group_ids, rewards, seq_ids, response_mask, new_logp, old_logp, ref_logp, hidden, cotangent, master)))


def solution(mesh):
    tokens = P(("rep", "shard"), None)
    return jax.shard_map(
        functools.partial(per_device, mesh.shape["rep"], mesh.shape["shard"]),
        mesh=mesh,
        in_specs=(tokens,) * 9 + (P(None, "shard", None),),
        out_specs=(P("shard", None), P(None, None, "shard")),
        check_vma=False,
    )
```

time: 118 us -> 92.1 us (0.78)
  the two profiles are of different devices: /device:TPU:0 before, /device:TPU:5 now
where the time goes in v1:
time: 92.1 us; the launch traced here: 91.9 us
  Pallas kernels  87.6 us (95%)
  local copies, waits for them, and re-layouts  3.67 us (4%)
    pallas_call x1, Pallas kernels, per_device(): pl.pallas_call(functools.partial(step_kernel, n_rep, n_shard, split, grou...  87.6 us
    unnamed x2, local copies, waits for them, and re-layouts  3.67 us

profile of v1, /device:TPU:5, one launch (start us, length us, event | category | flops | bytes accessed | tf_op | source)
XLA Modules:
  0.0 91.9 jit_solution(8335476480331957556)
XLA Ops:
  0.6 87.6 %step.1 = (f32[448,1024]{1,0:T(8,128)S(1)}, bf16[3,3584,256]{2,1,0:T(8,128)(2,1)S(1)}) custom-call(s32[1,4]{1,0:T(1,128)} %group_hbm.1, f32[1,4]{1,0:T(1,128)} %reward_hbm.1, s32[1,448]{1,0:T(1,128)} %args_0_.4, s32[1,448]{1,0:T(1,128)} %args_1_.4, f32[1,448]{1,0:T(1,128)} %args_2_.4, f32[1,448]{1,0:T(1,128)} %args_3_.4, f32[1,448]{1,0:T(1,128)} %args_4_.4, ...), custom_call_target="tpu_custom_call" | custom-call | tf_op jit(solution)/shard_map/step/pallas_call | solution.py:557
  88.3 1.2 %copy.14 = f32[448,1024]{1,0:T(8,128)} copy(f32[448,1024]{1,0:T(8,128)S(1)} %get-tuple-element.2) | data formatting | bytes 3670016
  89.5 2.4 %copy.15 = bf16[3,3584,256]{2,1,0:T(8,128)(2,1)} copy(bf16[3,3584,256]{2,1,0:T(8,128)(2,1)S(1)} %get-tuple-element.3) | data formatting | bytes 11010048

commit v2 on v1

--- a/solution.py
+++ b/solution.py
@@ -45,7 +45,7 @@
     hidden_ref, cot_ref, master_ref,
     nm_ref, roll_ref,
     group_ref, reward_ref, ids_in, logp_in, small, stat_in, square_in, info_in, info_own, token_own, token_in, hid, hid_t, cot, delta, part, sums, zin,
-    grad, grad_b, base_out, base_in, m0, stage_in, stage_out, rows_in,
+    grad, grad_b, relay_in, base_out, base_in, m0, stage_in, stage_out, rows_in,
     send_sems, recv_sems, local_sems, all_sems, set_send, set_recv,
 ):
     z_count = n_shard // 2
@@ -151,7 +151,12 @@
     quarter = r % split
     own_half = pl.ds(pl.multiple_of(core * half, LANES), half)
     other_half = pl.ds(pl.multiple_of((1 - core) * half, LANES), half)
-    fetch_stage = local(master_ref.at[pl.ds(1, layer_count - 1), span(quarter * sub, sub), :], stage_in, 0)
+    yi = quarter // 2
+    both = 2 if split == 4 else 1
+    quarters = [quarter, quarter + (1 - 2 * yi) * 2][:both]
+    fetch_stage = [
+        local(master_ref.at[pl.ds(1, layer_count - 1), span(q * sub, sub), :], stage_in.at[n], (0, 11)[n])
+        for n, q in enumerate(quarters)]
     fetch_hid = local(hidden_ref.at[:, own_half], hid.at[pl.ds(0, toks)], 1)
     fetch_cot = local(cot_ref, cot.at[0], 2)
     fetch_m0 = local(master_ref.at[0], m0, 3)
@@ -192,27 +197,8 @@
     mate_hid = send(hidden_ref.at[:, other_half], hid.at[pl.ds(toks, toks)], mate)
     mate_cot = send(cot_ref, cot.at[1], mate)
 
-    with jax.named_scope('w_stage'):
-        fetch_stage.wait()
-    for h in range(KV_HEADS):
-        low = KV_HEADS * HEAD + h * HEAD
-        for l in range(layer_count - 1):
-            stage_out[h, l, :, :HEAD] = stage_in[l, :, h * HEAD:(h + 1) * HEAD].astype(jnp.bfloat16)
-            stage_out[h, l, :, HEAD:] = stage_in[l, :, low:low + HEAD].astype(jnp.bfloat16)
-
     def block(z, xx, yy):
         return roll_ref.at[pl.ds(1, layer_count - 1), span((2 * z + xx) * rows + (2 * yy + core) * sub, sub), :]
-
-    yi = quarter // 2
-    xy = [(r, flip(s, 0)[0])]
-    first_at = (1 - x, yi)
-    if split == 4:
-        other = flip(r, 1)[0]
-        xy = [(r + core * (other - r), s + (1 - core) * (1 - 2 * x)),
-              (r + (1 - core) * (other - r), s + core * (1 - 2 * x))]
-        first_at = (x + (1 - core) * (1 - 2 * x), yi + core * (1 - 2 * yi))
-        second_at = (x + core * (1 - 2 * x), yi + (1 - core) * (1 - 2 * yi))
-        third_at = (1 - x, 1 - yi)
 
     near = [zi]
     for e in range(1, z_count):
@@ -221,23 +207,51 @@
             if e >> bit & 1:
                 z = flip(z, bit)[0]
         near.append(z)
-    m1 = [remote(stage_out.at[near[e] % KV_HEADS], block(zi, x, yi), (r, near[e] * 2 + x), numbered())
-          for e in range(1, z_count)]
-    for copy in m1:
-        copy.start()
-        started.append(copy)
-    roll_ref[1:, span((2 * zi + x) * rows + quarter * sub, sub), :] = stage_out[head]
-    SPREAD_0, SPREAD_1, FORWARD, TO_MATE, GATHER, PIECES, HALVES, GRADS, BASE = range(9)
+    beside = (r, flip(s, 0)[0])
+    above = (flip(r, 1)[0], s)
+    halves_at = [yi, 1 - yi]
+    m1 = []
+    for n in range(both):
+        with jax.named_scope('w_stage'):
+            fetch_stage[n].wait()
+        for h in range(KV_HEADS):
+            low = KV_HEADS * HEAD + h * HEAD
+            for l in range(layer_count - 1):
+                stage_out[n, h, l, :, :HEAD] = stage_in[n, l, :, h * HEAD:(h + 1) * HEAD].astype(jnp.bfloat16)
+                stage_out[n, h, l, :, HEAD:] = stage_in[n, l, :, low:low + HEAD].astype(jnp.bfloat16)
+        m1.append([send(stage_out.at[n, near[e] % KV_HEADS], block(zi, x, halves_at[n]), (r, near[e] * 2 + x))
+                   for e in range(1, z_count)])
+        roll_ref[1:, span((2 * zi + x) * rows + quarters[n] * sub, sub), :] = stage_out[n, head]
+
+    SPREAD, FORWARD, TO_MATE, GATHER, PIECES, HALVES, GRADS, BASE, RELAY = range(9)
     level_in = 9
+
+    spread_in = [numbered() for _ in range(z_count)]
+
+    def spread_copy(e):
+        here = block(near[e], x, yi)
+        return pltpu.make_async_remote_copy(
+            src_ref=here, dst_ref=here, send_sem=set_send.at[SPREAD], recv_sem=recv_sems.at[spread_in[e]],
+            device_id=beside, device_id_type=MESH)
 
     def spread_block(e):
         if e:
             with jax.named_scope(f'w_m1#{e}'):
-                m1[e - 1].wait_recv()
+                m1[0][e - 1].wait_recv()
+        spread_copy(e).start()
         here = block(near[e], x, yi)
-        for n, device in enumerate(xy):
-            put(here, here, device, SPREAD_0 + n, SPREAD_0 + n)
         put(here, here, mate, TO_MATE, TO_MATE)
+        if e == 0 and both == 2:
+            here = block(zi, x, 1 - yi)
+            put(here, here, beside, FORWARD, FORWARD)
+
+    def forward_block(e):
+        with jax.named_scope(f'w_sp#{e}'):
+            spread_copy(e).wait_recv()
+        got = block(near[e], 1 - x, yi)
+        if both == 2 and e:
+            put(got, got, above, FORWARD, FORWARD)
+        put(got, got, mate, TO_MATE, TO_MATE)
 
     spread_block(0)
 
@@ -280,6 +294,7 @@
     tokens = jnp.transpose(jnp.concatenate(
         [token_own[...], token_in[...], jnp.zeros((LANES - 16, padded), jnp.float32)], axis=0))[:toks]
 
+    spread_block(1)
     with jax.named_scope('w_stats'):
         stats.wait_recv()
     total = own_sums + jnp.sum(stat_in[...], axis=0)
@@ -311,13 +326,14 @@
     turns = [2, 1, 3, 0]
     order = [(head + d) % KV_HEADS for d in turns]
     tile = half // 2
-    inbound = {(i, k): numbered() for i in range(dims) for k in range(KV_HEADS)}
+    chunks = 2 * KV_HEADS
+    inbound = {(i, k): numbered() for i in range(dims) for k in range(chunks)}
 
     def halves(i, k):
         gone = offsets[i] + (1 - bits[i]) * lens[i + 1]
         return pltpu.make_async_remote_copy(
-            src_ref=part.at[order[k], span(gone, lens[i + 1])],
-            dst_ref=sums.at[order[k], pl.ds(starts[i], lens[i + 1])],
+            src_ref=part.at[order[k // 2], k % 2, span(gone, lens[i + 1])],
+            dst_ref=sums.at[order[k // 2], k % 2, pl.ds(starts[i], lens[i + 1])],
             send_sem=set_send.at[HALVES], recv_sem=recv_sems.at[inbound[i, k]],
             device_id=partners[i], device_id_type=MESH)
 
@@ -339,89 +355,124 @@
             for q in range(tile // final):
                 j = t * (tile // final) + q
                 place = spot(j, 0) + core * (spot(j, 1) - spot(j, 0))
-                part[h, span(place * final, final), :] = out[q * final:(q + 1) * final]
-        pass_on(0, k)
-        if k + 1 < KV_HEADS:
+                for side in range(2):
+                    part[h, side, span(place * final, final), :] = (
+                        out[q * final:(q + 1) * final, side * HEAD:(side + 1) * HEAD])
+        pass_on(0, 2 * k)
+        pass_on(0, 2 * k + 1)
+        if k in (1, 2) and k + 1 < z_count:
             spread_block(k + 1)
     for e in range(KV_HEADS, z_count):
         spread_block(e)
 
     inner = min(final, 112)
 
-    def add_in(i, h):
+    def add_in(i, k):
+        h, side = order[k // 2], k % 2
+
         @pl.loop(0, lens[i + 1] // inner)
         def _(t):
             at = span(offsets[i + 1] + t * inner, inner)
-            part[h, at, :] = (
-                part[h, at, :].astype(jnp.float32)
-                + sums[h, span(starts[i] + t * inner, inner), :].astype(jnp.float32)
+            part[h, side, at, :] = (
+                part[h, side, at, :].astype(jnp.float32)
+                + sums[h, side, span(starts[i] + t * inner, inner), :].astype(jnp.float32)
             ).astype(jnp.bfloat16)
 
     last = dims - 1
     mine = span(offsets[dims], final)
+    z_in = {(d, side): numbered() for side in range(2) for d in range(1, z_count)}
+
+    def z_copy(d, side):
+        return pltpu.make_async_remote_copy(
+            src_ref=part.at[(head + d) % KV_HEADS, side, mine], dst_ref=zin.at[d - 1, side],
+            send_sem=set_send.at[GRADS], recv_sem=recv_sems.at[z_in[d, side]],
+            device_id=z_peers[d], device_id_type=MESH)
 
     def z_send(k):
         for d in range(1, z_count):
-            if d % KV_HEADS == turns[k]:
-                put(part.at[order[k], mine], zin.at[d - 1], z_peers[d], GRADS, GRADS)
-
-    for t in range(KV_HEADS + last):
+            if d % KV_HEADS == turns[k // 2]:
+                z_copy(d, k % 2).start()
+
+    far = z_count > KV_HEADS
+    for t in range(chunks + last):
         for i in range(dims):
             k = t - i
-            if k < 0 or k >= KV_HEADS:
+            if k < 0 or k >= chunks:
                 continue
             with jax.named_scope(f'w_in#i={i}#k={k}'):
                 halves(i, k).wait_recv()
-            if i == last and k == KV_HEADS - 1 and z_count == KV_HEADS:
+            if i == last and k // 2 == KV_HEADS - 1 and not far:
+                side = k % 2
+                grad[:, side * HEAD:(side + 1) * HEAD] = (
+                    part[head, side, mine, :].astype(jnp.float32)
+                    + sums[head, side, pl.ds(starts[last], final), :].astype(jnp.float32))
                 continue
-            add_in(i, order[k])
+            add_in(i, k)
             if i < last:
                 pass_on(i + 1, k)
             else:
                 z_send(k)
-    with jax.named_scope('w_z'):
-        whole(zin, GRADS).wait_recv()
-
-    def gather_sum(t, acc):
-        g = part[head, span(offsets[dims] + t * inner, inner), :].astype(jnp.float32)
-        if z_count == KV_HEADS:
-            g = g + sums[head, span(starts[last] + t * inner, inner), :].astype(jnp.float32)
-        at = span(t * inner, inner)
-        for d in range(1, z_count):
-            g = g + zin[d - 1, at, :].astype(jnp.float32)
-        grad[at, :] = g
-        grad_b[at, :] = g.astype(jnp.bfloat16)
-        return acc + jnp.sum(g * g, axis=0, keepdims=True)
-
-    squares = lax.fori_loop(0, final // inner, gather_sum, jnp.zeros((1, WIDE), jnp.float32))
-    own_square = jnp.broadcast_to(jnp.sum(squares, axis=1, keepdims=True), (1, LANES))
+        if t == 2:
+            forward_block(0)
+            forward_block(1)
+        if t == 6 and z_count > 2:
+            forward_block(2)
+    if far:
+        for side in range(2):
+            grad[:, side * HEAD:(side + 1) * HEAD] = part[head, side, mine, :].astype(jnp.float32)
+
+    arrivals = [d for turn in turns for d in range(1, z_count) if d % KV_HEADS == turn]
+    own_square = jnp.zeros((1, HEAD), jnp.float32)
+    for d in arrivals:
+        for side in range(2):
+            with jax.named_scope(f'w_z#{d}'):
+                z_copy(d, side).wait_recv()
+            cut = slice(side * HEAD, (side + 1) * HEAD)
+            g = grad[:, cut] + zin[d - 1, side].astype(jnp.float32)
+            grad[:, cut] = g
+            if d == arrivals[-1]:
+                own_square = own_square + jnp.sum(g * g, axis=0, keepdims=True)
+                grad_b[:, cut] = g.astype(jnp.bfloat16)
+
+    own_square = jnp.broadcast_to(jnp.sum(own_square, axis=1, keepdims=True), (1, LANES))
     small[1, :, :LANES] = own_square
     all_squares = to_all(small.at[1, :, pl.ds(0, LANES)], square_in, 2)
 
+    relayed = n_rep == 4 and pieces == 1
+    y_other = flip(y, 0)[0] if relayed else y
+    other_z = home(y_other)[0]
     nm_numbers = [numbered() for _ in range(n_rep // 2)]
     nm_in = counter[0]
     counter[0] += KV_HEADS * pieces
-    nm_copies = []
-    for j in range(n_rep // 2):
-        copy = remote(
-            grad_b, rows_in.at[head, span(home_piece * final, final)], (2 * j + core, 2 * home_z + x),
-            nm_numbers[j], nm_in + head * pieces + home_piece)
-        leaves = (home_z // KV_HEADS == zi // KV_HEADS) & ((home_z != zi) | (j != y))
-        nm_copies.append((leaves, copy))
-        pl.when(leaves)(copy.start)
+    here_rows = rows_in.at[head, span(home_piece * final, final)]
+    if relayed:
+        put(grad_b, relay_in, above, RELAY, RELAY)
+        nm_copies = [
+            (home_z != zi, remote(grad_b, here_rows, (r, 2 * home_z + x), nm_numbers[0], nm_in + head)),
+            (other_z != zi, remote(relay_in, here_rows, (r, 2 * other_z + x), nm_numbers[1], nm_in + head))]
+        pl.when(home_z != zi)(nm_copies[0][1].start)
+    else:
+        nm_copies = []
+        for j in range(n_rep // 2):
+            copy = remote(
+                grad_b, here_rows, (2 * j + core, 2 * home_z + x),
+                nm_numbers[j], nm_in + head * pieces + home_piece)
+            leaves = (home_z // KV_HEADS == zi // KV_HEADS) & ((home_z != zi) | (j != y))
+            nm_copies.append((leaves, copy))
+            pl.when(leaves)(copy.start)
 
     @pl.when(is_home)
     def _():
         rows_in[head, span(home_piece * final, final), :] = grad_b[...]
 
-    blocks = roll_ref.at[pl.ds(1, layer_count - 1), pl.ds(0, z_count * sub), :]
-    with jax.named_scope('w_sp0'):
-        whole(blocks, SPREAD_0).wait_recv()
-    for z in near:
-        got = block(z, *first_at)
-        if split == 4:
-            put(got, got, xy[1], FORWARD, FORWARD)
-        put(got, got, mate, TO_MATE, TO_MATE)
+    for e in range(3 if z_count > 2 else 2, z_count):
+        forward_block(e)
+    if both == 2:
+        for e in range(z_count):
+            if e:
+                m1[1][e - 1].wait_recv()
+            got = block(near[e], x, 1 - yi)
+            put(got, got, mate, TO_MATE, TO_MATE)
 
     @pl.when(home_z != zi)
     def _():
@@ -454,6 +505,14 @@
             put(layer0(*at), layer0(*at), mate, PIECES, PIECES)
         passed = len(have)
         have = have + [across(*at, i) for at in have]
+        if i == last and relayed:
+            with jax.named_scope('w_relay'):
+                whole(relay_in, RELAY).wait_recv()
+            pl.when(other_z != zi)(nm_copies[1][1].start)
+
+            @pl.when(other_z == zi)
+            def _():
+                rows_in[head] = relay_in[...]
         if i:
             with jax.named_scope(f'w_ag#{i}'):
                 gather_in(i).wait_recv()
@@ -473,20 +532,18 @@
         low = zi + core * (z_count - 1 - 2 * zi)
         for h in range(KV_HEADS):
             for p in range(pieces):
-                @pl.when((h != head) | (y != low * pieces + p))
+                @pl.when((h != head) if relayed else (h != head) | (y != low * pieces + p))
                 def _():
                     landed(h, p).wait_recv()
             hand_over[h].start()
 
-    if split == 4:
-        with jax.named_scope('w_sp1'):
-            whole(blocks, SPREAD_1).wait_recv()
+    blocks = roll_ref.at[pl.ds(1, layer_count - 1), pl.ds(0, z_count * sub), :]
+    if both == 2:
         with jax.named_scope('w_fwd'):
             whole(blocks, FORWARD).wait_recv()
         for z in near:
-            for there in (second_at, third_at):
-                got = block(z, *there)
-                put(got, got, mate, TO_MATE, TO_MATE)
+            got = block(z, 1 - x, 1 - yi)
+            put(got, got, mate, TO_MATE, TO_MATE)
     with jax.named_scope('w_gathered'):
         gather_in(0).wait_recv()
     for at in have[passed:]:
@@ -523,14 +580,15 @@
         pl.when(leaves)(copy.wait_send)
     for copy in started:
         copy.wait_send()
-    whole(blocks, SPREAD_0).wait_send()
-    if split == 4:
-        whole(blocks, SPREAD_1).wait_send()
+    whole(blocks, SPREAD).wait_send()
+    if both == 2:
         whole(blocks, FORWARD).wait_send()
+    if relayed:
+        whole(relay_in, RELAY).wait_send()
     whole(all_blocks, TO_MATE).wait_send()
     whole(all_pieces, PIECES).wait_send()
     whole(roll_ref.at[0, pl.ds(0, (n_rep - 1) * final), :], GATHER).wait_send()
-    whole(part.at[:, pl.ds(0, half - final), :], HALVES).wait_send()
+    whole(part.at[:, :, pl.ds(0, half - final), :], HALVES).wait_send()
     whole(zin, GRADS).wait_send()
     stats.wait_send()
     all_squares.wait_send()
@@ -575,16 +633,17 @@
             pltpu.VMEM((half, 2 * toks), bf16),
             pltpu.VMEM((2, toks, cols), bf16),
             pltpu.VMEM((2 * toks, WIDE), bf16),
-            pltpu.VMEM((KV_HEADS, half, WIDE), bf16),
-            pltpu.VMEM((KV_HEADS, half, WIDE), bf16),
-            pltpu.VMEM((z_count - 1, final, WIDE), bf16),
+            pltpu.VMEM((KV_HEADS, 2, half, HEAD), bf16),
+            pltpu.VMEM((KV_HEADS, 2, half, HEAD), bf16),
+            pltpu.VMEM((z_count - 1, 2, final, HEAD), bf16),
             pltpu.VMEM((final, WIDE), f32),
+            pltpu.VMEM((final, WIDE), bf16),
             pltpu.VMEM((final, WIDE), bf16),
             pltpu.VMEM((KV_HEADS, final, WIDE), bf16),
             pltpu.VMEM((final, WIDE), bf16),
             pltpu.VMEM((rows, cols), f32),
-            pltpu.VMEM((layer_count - 1, sub, cols), f32),
-            pltpu.VMEM((KV_HEADS, layer_count - 1, sub, WIDE), bf16),
+            pltpu.VMEM((2, layer_count - 1, sub, cols), f32),
+            pltpu.VMEM((2, KV_HEADS, layer_count - 1, sub, WIDE), bf16),
             pltpu.VMEM((KV_HEADS, rows, WIDE), bf16),
             pltpu.SemaphoreType.DMA((sem_count,)),
             pltpu.SemaphoreType.DMA((sem_count,)),

time: 92.1 us -> 81.9 us (0.89)
  the two profiles are of different devices: /device:TPU:5 before, /device:TPU:0 now
where the time goes in v2:
time: 81.9 us; the launch traced here: 81.7 us
  Pallas kernels  77.4 us (95%)
  local copies, waits for them, and re-layouts  3.67 us (4%)
    pallas_call x1, Pallas kernels, per_device(): pl.pallas_call(functools.partial(step_kernel, n_rep, n_shard, split, grou...  77.4 us
    unnamed x2, local copies, waits for them, and re-layouts  3.67 us

profile of v2, /device:TPU:0, one launch (start us, length us, event | category | flops | bytes accessed | tf_op | source)
XLA Modules:
  0.0 81.7 jit_solution(11308544142190214130)
XLA Ops:
  0.6 77.4 %step.1 = (f32[448,1024]{1,0:T(8,128)S(1)}, bf16[3,3584,256]{2,1,0:T(8,128)(2,1)S(1)}) custom-call(s32[1,4]{1,0:T(1,128)} %group_hbm.1, f32[1,4]{1,0:T(1,128)} %reward_hbm.1, s32[1,448]{1,0:T(1,128)} %args_0_.4, s32[1,448]{1,0:T(1,128)} %args_1_.4, f32[1,448]{1,0:T(1,128)} %args_2_.4, f32[1,448]{1,0:T(1,128)} %args_3_.4, f32[1,448]{1,0:T(1,128)} %args_4_.4, ...), custom_call_target="tpu_custom_call" | custom-call | tf_op jit(solution)/shard_map/step/pallas_call | solution.py:615
  78.0 1.2 %copy.14 = f32[448,1024]{1,0:T(8,128)} copy(f32[448,1024]{1,0:T(8,128)S(1)} %get-tuple-element.2) | data formatting | bytes 3670016
  79.3 2.4 %copy.15 = bf16[3,3584,256]{2,1,0:T(8,128)(2,1)} copy(bf16[3,3584,256]{2,1,0:T(8,128)(2,1)S(1)} %get-tuple-element.3) | data formatting | bytes 11010048

commit v3 on v2

--- a/solution.py
+++ b/solution.py
@@ -46,7 +46,7 @@
     nm_ref, roll_ref,
     group_ref, reward_ref, ids_in, logp_in, small, stat_in, square_in, info_in, info_own, token_own, token_in, hid, hid_t, cot, delta, part, sums, zin,
     grad, grad_b, relay_in, base_out, base_in, m0, stage_in, stage_out, rows_in,
-    send_sems, recv_sems, local_sems, all_sems, set_send, set_recv,
+    local_sems, all_sems, set_send, set_recv,
 ):
     z_count = n_shard // 2
     dims = n_rep.bit_length() - 1
@@ -63,34 +63,29 @@
     pieces = rows // final
     half_z = z_count // 2
     counter = [0]
-    started = []
+    (SPREAD, FORWARD, TO_MATE, PIECES, BASE, RELAY, HAND,
+     MASTERS, GATHER, HALVES, GRADS, RETURN) = range(12)
+    given_in, given_out = 7, 12
+    mate = (flip(r, 0)[0], s)
 
     def numbered():
-        number = counter[0]
+        number = given_in + counter[0]
         counter[0] += 1
         return number
 
-    def remote(src, dst, device, number, landing=None):
+    def copy_to(src, dst, device, gone, landed):
         return pltpu.make_async_remote_copy(
-            src_ref=src, dst_ref=dst, send_sem=send_sems.at[number],
-            recv_sem=recv_sems.at[number if landing is None else landing],
+            src_ref=src, dst_ref=dst, send_sem=set_send.at[gone], recv_sem=set_recv.at[landed],
             device_id=device, device_id_type=MESH)
 
-    def send(src, dst, device):
-        copy = remote(src, dst, device, numbered())
-        copy.start()
-        started.append(copy)
-        return copy
-
     def put(src, dst, device, gone, landed):
-        pltpu.make_async_remote_copy(
-            src_ref=src, dst_ref=dst, send_sem=set_send.at[gone], recv_sem=set_recv.at[landed],
-            device_id=device, device_id_type=MESH).start()
+        copy_to(src, dst, device, gone, landed).start()
 
     def whole(ref, number):
-        return pltpu.make_async_remote_copy(
-            src_ref=ref, dst_ref=ref, send_sem=set_send.at[number], recv_sem=set_recv.at[number],
-            device_id=(flip(r, 0)[0], s), device_id_type=MESH)
+        return copy_to(ref, ref, mate, number, number)
+
+    def landing(ref, number):
+        return copy_to(ref, ref, mate, 0, number)
 
     def local(src, dst, number):
         copy = pltpu.make_async_copy(src, dst, local_sems.at[number])
@@ -112,7 +107,6 @@
             src_ref=dst, dst_ref=dst, send_sem=all_sems.at[sem], recv_sem=all_sems.at[sem + 1],
             device_id=(flip(r, 0)[0], s), device_id_type=MESH)
 
-    mate = (flip(r, 0)[0], s)
     options = []
     for bit in range(1, dims):
         other, here = flip(r, bit)
@@ -193,9 +187,14 @@
         pl.semaphore_wait(barrier, everyone - 1)
 
     stats = to_all(small.at[0], stat_in, 0)
-    mate_info = send(info_own, info_in, mate)
-    mate_hid = send(hidden_ref.at[:, other_half], hid.at[pl.ds(toks, toks)], mate)
-    mate_cot = send(cot_ref, cot.at[1], mate)
+    sent_out = n_rep // 2 + given_out
+    mate_copies = [
+        copy_to(src, dst, mate, sent_out + n, numbered()) for n, (src, dst) in enumerate((
+            (info_own, info_in), (hidden_ref.at[:, other_half], hid.at[pl.ds(toks, toks)]), (cot_ref, cot.at[1]),
+            (token_own, token_in)))]
+    mate_info, mate_hid, mate_cot, mate_tok = mate_copies
+    for copy in mate_copies[:3]:
+        copy.start()
 
     def block(z, xx, yy):
         return roll_ref.at[pl.ds(1, layer_count - 1), span((2 * z + xx) * rows + (2 * yy + core) * sub, sub), :]
@@ -210,8 +209,12 @@
     beside = (r, flip(s, 0)[0])
     above = (flip(r, 1)[0], s)
     halves_at = [yi, 1 - yi]
-    m1 = []
-    for n in range(both):
+    m1 = [[numbered() for _ in range(1, z_count)] for _ in range(both)]
+
+    def master_in(n, e):
+        return landing(block(zi, x, halves_at[n]), m1[n][e - 1])
+
+    def stage_masters(n):
         with jax.named_scope('w_stage'):
             fetch_stage[n].wait()
         for h in range(KV_HEADS):
@@ -219,37 +222,34 @@
             for l in range(layer_count - 1):
                 stage_out[n, h, l, :, :HEAD] = stage_in[n, l, :, h * HEAD:(h + 1) * HEAD].astype(jnp.bfloat16)
                 stage_out[n, h, l, :, HEAD:] = stage_in[n, l, :, low:low + HEAD].astype(jnp.bfloat16)
-        m1.append([send(stage_out.at[n, near[e] % KV_HEADS], block(zi, x, halves_at[n]), (r, near[e] * 2 + x))
-                   for e in range(1, z_count)])
         roll_ref[1:, span((2 * zi + x) * rows + quarters[n] * sub, sub), :] = stage_out[n, head]
 
-    SPREAD, FORWARD, TO_MATE, GATHER, PIECES, HALVES, GRADS, BASE, RELAY = range(9)
-    level_in = 9
-
+    def send_masters(n, which):
+        for e in which:
+            put(stage_out.at[n, near[e] % KV_HEADS], block(zi, x, halves_at[n]), (r, near[e] * 2 + x),
+                MASTERS, m1[n][e - 1])
+
+    stage_masters(0)
+    send_masters(0, range(1, z_count))
     spread_in = [numbered() for _ in range(z_count)]
 
-    def spread_copy(e):
-        here = block(near[e], x, yi)
-        return pltpu.make_async_remote_copy(
-            src_ref=here, dst_ref=here, send_sem=set_send.at[SPREAD], recv_sem=recv_sems.at[spread_in[e]],
-            device_id=beside, device_id_type=MESH)
+    def second_block(e, device):
+        here = block(near[e], x, 1 - yi)
+        put(here, here, device, FORWARD, FORWARD)
 
     def spread_block(e):
         if e:
             with jax.named_scope(f'w_m1#{e}'):
-                m1[0][e - 1].wait_recv()
-        spread_copy(e).start()
+                master_in(0, e).wait_recv()
         here = block(near[e], x, yi)
+        put(here, here, beside, SPREAD, spread_in[e])
         put(here, here, mate, TO_MATE, TO_MATE)
-        if e == 0 and both == 2:
-            here = block(zi, x, 1 - yi)
-            put(here, here, beside, FORWARD, FORWARD)
-
-    def forward_block(e):
+
+    def forward_block(e, up):
+        got = block(near[e], 1 - x, yi)
         with jax.named_scope(f'w_sp#{e}'):
-            spread_copy(e).wait_recv()
-        got = block(near[e], 1 - x, yi)
-        if both == 2 and e:
+            landing(got, spread_in[e]).wait_recv()
+        if up:
             put(got, got, above, FORWARD, FORWARD)
         put(got, got, mate, TO_MATE, TO_MATE)
 
@@ -260,7 +260,10 @@
     terms = token_rows(ids_in[0:1], ids_in[1:2], logp_in[0:1], logp_in[1:2], logp_in[2:3])
     for j, row in enumerate(terms):
         token_own[j:j + 1, :toks] = row
-    mate_tok = send(token_own, token_in, mate)
+    mate_tok.start()
+    if both == 2:
+        stage_masters(1)
+        second_block(0, beside)
 
     is_home = home_z == zi
     fetch_m0.wait()
@@ -290,11 +293,6 @@
     mate_cot.wait_recv()
     mate_info.wait_recv()
     mate_tok.wait_recv()
-    padded = token_own.shape[1]
-    tokens = jnp.transpose(jnp.concatenate(
-        [token_own[...], token_in[...], jnp.zeros((LANES - 16, padded), jnp.float32)], axis=0))[:toks]
-
-    spread_block(1)
     with jax.named_scope('w_stats'):
         stats.wait_recv()
     total = own_sums + jnp.sum(stat_in[...], axis=0)
@@ -304,16 +302,16 @@
     spread_of = jnp.maximum(
         jnp.sqrt(jnp.maximum(pltpu.roll(total, wide - 2 * groups, 1) / count - mean * mean, 0.0)), 0.5)
 
-    def coef_of(told, low):
+    def coef_of(told, token):
         hots, given = told[:SEQ_DEV], told[SEQ_DEV:, 0:1]
         advantage = (given - jnp.sum(hots * mean, axis=1, keepdims=True)) / jnp.sum(
             hots * spread_of, axis=1, keepdims=True)
-        out = tokens[:, low + SEQ_DEV:low + SEQ_DEV + 1]
+        out = token[SEQ_DEV:SEQ_DEV + 1]
         for j in range(SEQ_DEV):
-            out = out + tokens[:, low + j:low + j + 1] * advantage[j:j + 1, :]
-        return out
-
-    coefs = [coef_of(info, 0), coef_of(info_in[...], 8)]
+            out = out + token[j:j + 1] * advantage[j:j + 1]
+        return jnp.transpose(jnp.broadcast_to(out, (LANES, out.shape[1])))[:toks]
+
+    coefs = [coef_of(info, token_own[...]), coef_of(info_in[...], token_in[...])]
 
     lens, offsets = [half], [0]
     for i in range(dims):
@@ -334,7 +332,7 @@
         return pltpu.make_async_remote_copy(
             src_ref=part.at[order[k // 2], k % 2, span(gone, lens[i + 1])],
             dst_ref=sums.at[order[k // 2], k % 2, pl.ds(starts[i], lens[i + 1])],
-            send_sem=set_send.at[HALVES], recv_sem=recv_sems.at[inbound[i, k]],
+            send_sem=set_send.at[HALVES], recv_sem=set_recv.at[inbound[i, k]],
             device_id=partners[i], device_id_type=MESH)
 
     def pass_on(i, k):
@@ -360,10 +358,10 @@
                         out[q * final:(q + 1) * final, side * HEAD:(side + 1) * HEAD])
         pass_on(0, 2 * k)
         pass_on(0, 2 * k + 1)
-        if k in (1, 2) and k + 1 < z_count:
-            spread_block(k + 1)
-    for e in range(KV_HEADS, z_count):
-        spread_block(e)
+        if k == 0:
+            spread_block(1)
+    if both == 2:
+        send_masters(1, [e for e in range(1, z_count) if e != 2])
 
     inner = min(final, 112)
 
@@ -385,7 +383,7 @@
     def z_copy(d, side):
         return pltpu.make_async_remote_copy(
             src_ref=part.at[(head + d) % KV_HEADS, side, mine], dst_ref=zin.at[d - 1, side],
-            send_sem=set_send.at[GRADS], recv_sem=recv_sems.at[z_in[d, side]],
+            send_sem=set_send.at[GRADS], recv_sem=set_recv.at[z_in[d, side]],
             device_id=z_peers[d], device_id_type=MESH)
 
     def z_send(k):
@@ -412,11 +410,11 @@
                 pass_on(i + 1, k)
             else:
                 z_send(k)
-        if t == 2:
-            forward_block(0)
-            forward_block(1)
-        if t == 6 and z_count > 2:
-            forward_block(2)
+        if t == 5:
+            forward_block(0, False)
+            forward_block(1, both == 2)
+        if t == chunks - 2 and both == 2 and z_count > 2:
+            send_masters(1, [2])
     if far:
         for side in range(2):
             grad[:, side * HEAD:(side + 1) * HEAD] = part[head, side, mine, :].astype(jnp.float32)
@@ -439,24 +437,30 @@
     all_squares = to_all(small.at[1, :, pl.ds(0, LANES)], square_in, 2)
 
     relayed = n_rep == 4 and pieces == 1
+    relay_at = [numbered(), numbered()]
     y_other = flip(y, 0)[0] if relayed else y
     other_z = home(y_other)[0]
-    nm_numbers = [numbered() for _ in range(n_rep // 2)]
-    nm_in = counter[0]
-    counter[0] += KV_HEADS * pieces
+    nm_in = [numbered() for _ in range(KV_HEADS * pieces)][0]
     here_rows = rows_in.at[head, span(home_piece * final, final)]
     if relayed:
-        put(grad_b, relay_in, above, RELAY, RELAY)
+        for u in range(2):
+            cut = pl.ds(u * (final // 2), final // 2)
+            put(grad_b.at[cut], relay_in.at[cut], above, RELAY, relay_at[u])
         nm_copies = [
-            (home_z != zi, remote(grad_b, here_rows, (r, 2 * home_z + x), nm_numbers[0], nm_in + head)),
-            (other_z != zi, remote(relay_in, here_rows, (r, 2 * other_z + x), nm_numbers[1], nm_in + head))]
+            (home_z != zi, copy_to(grad_b, here_rows, (r, 2 * home_z + x), RETURN, nm_in + head)),
+            (other_z != zi, copy_to(relay_in, here_rows, (r, 2 * other_z + x), RETURN + 1, nm_in + head))]
+        relay_out = [
+            copy_to(relay_in.at[pl.ds(u * (final // 2), final // 2)],
+                    rows_in.at[head, pl.ds(u * (final // 2), final // 2)],
+                    (r, 2 * other_z + x), RETURN + 1, nm_in + head)
+            for u in range(2)]
         pl.when(home_z != zi)(nm_copies[0][1].start)
     else:
         nm_copies = []
         for j in range(n_rep // 2):
-            copy = remote(
+            copy = copy_to(
                 grad_b, here_rows, (2 * j + core, 2 * home_z + x),
-                nm_numbers[j], nm_in + head * pieces + home_piece)
+                RETURN + j, nm_in + head * pieces + home_piece)
             leaves = (home_z // KV_HEADS == zi // KV_HEADS) & ((home_z != zi) | (j != y))
             nm_copies.append((leaves, copy))
             pl.when(leaves)(copy.start)
@@ -465,14 +469,12 @@
     def _():
         rows_in[head, span(home_piece * final, final), :] = grad_b[...]
 
-    for e in range(3 if z_count > 2 else 2, z_count):
-        forward_block(e)
+    for e in range(2, z_count):
+        spread_block(e)
     if both == 2:
-        for e in range(z_count):
-            if e:
-                m1[1][e - 1].wait_recv()
-            got = block(near[e], x, 1 - yi)
-            put(got, got, mate, TO_MATE, TO_MATE)
+        for e in range(3, z_count):
+            master_in(1, e).wait_recv()
+            second_block(e, beside)
 
     @pl.when(home_z != zi)
     def _():
@@ -491,40 +493,57 @@
         roll_ref[0, span(row_me + t * inner, inner), :] = (
             base_in[at, :].astype(jnp.float32) - scale * grad[at, :]).astype(jnp.bfloat16)
 
-    def layer0(yy, xx):
-        return roll_ref.at[0, span(row_of(yy, xx), final), :]
-
-    def gather_in(i):
-        return whole(roll_ref.at[0, pl.ds(0, final << (dims - 1 - i)), :], level_in + i)
-
-    have, passed = [(y, x)], 0
+    parts = 2 if final // 2 % SUB == 0 else 1
+    size = final // parts
+    level_in = [[numbered() for _ in range(parts)] for _ in range(dims)]
+
+    def layer0(yy, xx, u):
+        return roll_ref.at[0, span(row_of(yy, xx) + u * size, size), :]
+
+    def gather_in(i, u):
+        return landing(roll_ref.at[0, pl.ds(0, size << (dims - 1 - i)), :], level_in[i][u])
+
+    def gather_out(i, u):
+        for at in have[:1 << (last - i)]:
+            here = layer0(*at, u)
+            put(here, here, partners[i], GATHER, level_in[i][u])
+
+    def piece_out(at):
+        for u in range(parts):
+            here = layer0(*at, u)
+            put(here, here, mate, PIECES, PIECES)
+
+    have = [(y, x)]
     for i in reversed(range(dims)):
-        for at in have:
-            put(layer0(*at), layer0(*at), partners[i], GATHER, level_in + i)
-        for at in have[passed:]:
-            put(layer0(*at), layer0(*at), mate, PIECES, PIECES)
-        passed = len(have)
         have = have + [across(*at, i) for at in have]
-        if i == last and relayed:
+    for u in range(parts):
+        gather_out(last, u)
+    piece_out(have[0])
+    if relayed:
+        for u in range(2):
             with jax.named_scope('w_relay'):
-                whole(relay_in, RELAY).wait_recv()
-            pl.when(other_z != zi)(nm_copies[1][1].start)
-
-            @pl.when(other_z == zi)
-            def _():
-                rows_in[head] = relay_in[...]
-        if i:
-            with jax.named_scope(f'w_ag#{i}'):
-                gather_in(i).wait_recv()
+                landing(relay_in.at[pl.ds(u * (final // 2), final // 2)], relay_at[u]).wait_recv()
+            pl.when(other_z != zi)(relay_out[u].start)
+
+        @pl.when(other_z == zi)
+        def _():
+            rows_in[head] = relay_in[...]
+    if z_count > 2:
+        forward_block(2, both == 2)
+    for i in reversed(range(last)):
+        for u in range(parts):
+            with jax.named_scope(f'w_ag#{i + 1}#{u}'):
+                gather_in(i + 1, u).wait_recv()
+            gather_out(i, u)
+        for at in have[1 << (last - 1 - i):1 << (last - i)]:
+            piece_out(at)
 
     keeper = zi // half_z
-    pass_number = [numbered() for _ in range(KV_HEADS)]
-    hand_over = [remote(rows_in.at[h], rows_in.at[h], mate, pass_number[h]) for h in range(KV_HEADS)]
+    hand_in = [numbered() for _ in range(KV_HEADS)]
+    hand_over = [copy_to(rows_in.at[h], rows_in.at[h], mate, HAND, hand_in[h]) for h in range(KV_HEADS)]
 
     def landed(h, p):
-        return remote(
-            rows_in.at[h, pl.ds(p * final, final)], rows_in.at[h, pl.ds(p * final, final)], mate,
-            nm_numbers[0], nm_in + h * pieces + p)
+        return landing(rows_in.at[h, pl.ds(p * final, final)], nm_in + h * pieces + p)
 
     @pl.when(core == keeper)
     @jax.named_scope('w_rows')
@@ -538,16 +557,24 @@
             hand_over[h].start()
 
     blocks = roll_ref.at[pl.ds(1, layer_count - 1), pl.ds(0, z_count * sub), :]
+    for e in range(3, z_count):
+        forward_block(e, False)
     if both == 2:
+        for e in range(1, min(z_count, 3)):
+            with jax.named_scope(f'w_m2#{e}'):
+                master_in(1, e).wait_recv()
         with jax.named_scope('w_fwd'):
             whole(blocks, FORWARD).wait_recv()
         for z in near:
-            got = block(z, 1 - x, 1 - yi)
-            put(got, got, mate, TO_MATE, TO_MATE)
+            for xx in (x, 1 - x):
+                got = block(z, xx, 1 - yi)
+                put(got, got, mate, TO_MATE, TO_MATE)
     with jax.named_scope('w_gathered'):
-        gather_in(0).wait_recv()
-    for at in have[passed:]:
-        put(layer0(*at), layer0(*at), mate, PIECES, PIECES)
+        for u in range(parts):
+            gather_in(0, u).wait_recv()
+            for at in have[n_rep // 2:]:
+                here = layer0(*at, u)
+                put(here, here, mate, PIECES, PIECES)
 
     @pl.when(core != keeper)
     @jax.named_scope('w_hand')
@@ -569,8 +596,7 @@
 
     @pl.when(core == keeper)
     def _():
-        for copy in hand_over:
-            copy.wait_send()
+        whole(rows_in, HAND).wait_send()
 
     @pl.when(is_home)
     def _():
@@ -578,8 +604,9 @@
 
     for leaves, copy in nm_copies:
         pl.when(leaves)(copy.wait_send)
-    for copy in started:
+    for copy in mate_copies:
         copy.wait_send()
+    whole(roll_ref.at[pl.ds(1, layer_count - 1), pl.ds(0, (z_count - 1) * both * sub), :], MASTERS).wait_send()
     whole(blocks, SPREAD).wait_send()
     if both == 2:
         whole(blocks, FORWARD).wait_send()
@@ -611,7 +638,9 @@
     pad = -(-toks // LANES) * LANES
     bf16, f32 = jnp.bfloat16, jnp.float32
     vmem, hbm = pl.BlockSpec(memory_space=pltpu.VMEM), pl.BlockSpec(memory_space=pltpu.HBM)
-    sem_count = 96 + 12 * z_count + 6 * n_rep
+    dims = n_rep.bit_length() - 1
+    both = 2 if split == 4 else 1
+    landings = 7 + 4 + 2 + KV_HEADS + both * (z_count - 1) + z_count + 8 * dims + 2 * (z_count - 1) + KV_HEADS * (n_rep // z_count) + 2 * dims
     return pl.pallas_call(
         functools.partial(step_kernel, n_rep, n_shard, split, groups),
         out_shape=(pltpu.VMEM((rows, cols), f32), pltpu.VMEM((layer_count, features, WIDE), bf16)),
@@ -645,12 +674,10 @@
             pltpu.VMEM((2, layer_count - 1, sub, cols), f32),
             pltpu.VMEM((2, KV_HEADS, layer_count - 1, sub, WIDE), bf16),
             pltpu.VMEM((KV_HEADS, rows, WIDE), bf16),
-            pltpu.SemaphoreType.DMA((sem_count,)),
-            pltpu.SemaphoreType.DMA((sem_count,)),
             pltpu.SemaphoreType.DMA((12,)),
             pltpu.SemaphoreType.DMA((4,)),
-            pltpu.SemaphoreType.DMA((12 + n_rep,)),
-            pltpu.SemaphoreType.DMA((12 + n_rep,)),
+            pltpu.SemaphoreType.DMA((16 + n_rep // 2,)),
+            pltpu.SemaphoreType.DMA((landings,)),
         ],
         compiler_params=pltpu.CompilerParams(
             collective_id=0, has_side_effects=True, vmem_limit_bytes=44 * 2**20

time: 81.9 us -> 77.8 us (0.950)
  the two profiles are of different devices: /device:TPU:0 before, /device:TPU:13 now
where the time goes in v3:
time: 77.8 us; the launch traced here: 77.7 us
  Pallas kernels  73.4 us (94%)
  local copies, waits for them, and re-layouts  3.67 us (5%)
    pallas_call x1, Pallas kernels, per_device(): pl.pallas_call(functools.partial(step_kernel, n_rep, n_shard, split, grou...  73.4 us
    unnamed x2, local copies, waits for them, and re-layouts  3.67 us

profile of v3, /device:TPU:13, one launch (start us, length us, event | category | flops | bytes accessed | tf_op | source)
XLA Modules:
  0.0 77.7 jit_solution(4307253959741241133)
XLA Ops:
  0.6 73.4 %step.1 = (f32[448,1024]{1,0:T(8,128)S(1)}, bf16[3,3584,256]{2,1,0:T(8,128)(2,1)S(1)}) custom-call(s32[1,4]{1,0:T(1,128)} %group_hbm.1, f32[1,4]{1,0:T(1,128)} %reward_hbm.1, s32[1,448]{1,0:T(1,128)} %args_0_.4, s32[1,448]{1,0:T(1,128)} %args_1_.4, f32[1,448]{1,0:T(1,128)} %args_2_.4, f32[1,448]{1,0:T(1,128)} %args_3_.4, f32[1,448]{1,0:T(1,128)} %args_4_.4, ...), custom_call_target="tpu_custom_call" | custom-call | tf_op jit(solution)/shard_map/step/pallas_call | solution.py:644
  74.0 1.2 %copy.14 = f32[448,1024]{1,0:T(8,128)} copy(f32[448,1024]{1,0:T(8,128)S(1)} %get-tuple-element.2) | data formatting | bytes 3670016
  75.2 2.4 %copy.15 = bf16[3,3584,256]{2,1,0:T(8,128)(2,1)} copy(bf16[3,3584,256]{2,1,0:T(8,128)(2,1)S(1)} %get-tuple-element.3) | data formatting | bytes 11010048

commit v4 on v3

--- a/solution.py
+++ b/solution.py
@@ -250,7 +250,9 @@
         with jax.named_scope(f'w_sp#{e}'):
             landing(got, spread_in[e]).wait_recv()
         if up:
-            put(got, got, above, FORWARD, FORWARD)
+            @pl.when(core == 0)
+            def _():
+                put(got, got, above, FORWARD, FORWARD)
         put(got, got, mate, TO_MATE, TO_MATE)
 
     spread_block(0)
@@ -323,6 +325,12 @@
         at += length
     turns = [2, 1, 3, 0]
     order = [(head + d) % KV_HEADS for d in turns]
+    paired = z_count == KV_HEADS
+    pair_z = flip(zi, 0)[0]
+    inner_plane = (zi + 1) // 2 % 2 == 1
+    if paired:
+        outer_z = (1 - zi // 2) * 3
+        order = [outer_z, flip(outer_z, 0)[0], pair_z, zi]
     tile = half // 2
     chunks = 2 * KV_HEADS
     inbound = {(i, k): numbered() for i in range(dims) for k in range(chunks)}
@@ -338,6 +346,17 @@
     def pass_on(i, k):
         halves(i, k).start()
 
+    def multiply_at(h, top, n):
+        where = [[[spot(j, c) for j in range(n_rep)].index(b * (n_rep // 2) + n) for b in range(2)] for c in range(2)]
+        (a, b), (a1, b1) = where
+        low, high = a + core * (a1 - a), b + core * (b1 - b)
+        out = jnp.dot(
+            hid_t[span((low + top * (high - low)) * final, final), :], delta[...], preferred_element_type=jnp.float32
+        ).astype(jnp.bfloat16)
+        at = span((top * (n_rep // 2) + n) * final, final)
+        for side in range(2):
+            part[h, side, at, :] = out[:, side * HEAD:(side + 1) * HEAD]
+
     for k in range(KV_HEADS):
         h = order[k]
         for side in range(2):
@@ -345,6 +364,14 @@
             for src in range(2):
                 delta[src * toks:(src + 1) * toks, side * HEAD:(side + 1) * HEAD] = (
                     coefs[src] * cot[src, :, low].astype(jnp.float32)).astype(jnp.bfloat16)
+        if k == 0:
+            for stays in (0, 1):
+                for n in range(n_rep // 2):
+                    multiply_at(h, bits[0] if stays else 1 - bits[0], n)
+                if not stays:
+                    pass_on(0, 0)
+                    pass_on(0, 1)
+            continue
         for t in range(2):
           with jax.named_scope(f'mul#k={k}'):
             out = jnp.dot(
@@ -358,8 +385,7 @@
                         out[q * final:(q + 1) * final, side * HEAD:(side + 1) * HEAD])
         pass_on(0, 2 * k)
         pass_on(0, 2 * k + 1)
-        if k == 0:
-            spread_block(1)
+    spread_block(1)
     if both == 2:
         send_masters(1, [e for e in range(1, z_count) if e != 2])
 
@@ -378,21 +404,58 @@
 
     last = dims - 1
     mine = span(offsets[dims], final)
-    z_in = {(d, side): numbered() for side in range(2) for d in range(1, z_count)}
-
-    def z_copy(d, side):
-        return pltpu.make_async_remote_copy(
-            src_ref=part.at[(head + d) % KV_HEADS, side, mine], dst_ref=zin.at[d - 1, side],
-            send_sem=set_send.at[GRADS], recv_sem=set_recv.at[z_in[d, side]],
-            device_id=z_peers[d], device_id_type=MESH)
+    sources = range(2) if paired else range(z_count - 1)
+    z_in = {(n, side): numbered() for side in range(2) for n in sources}
+    z_mid = [numbered() for _ in range(4)] if paired else []
+
+    def z_put(k, landing_ref, number, z):
+        put(part.at[order[k // 2], k % 2, mine], landing_ref, (r, 2 * z + x), GRADS, number)
 
     def z_send(k):
-        for d in range(1, z_count):
-            if d % KV_HEADS == turns[k // 2]:
-                z_copy(d, k % 2).start()
+        if not paired:
+            for d in range(1, z_count):
+                if d % KV_HEADS == turns[k // 2]:
+                    z_put(k, zin.at[d - 1, k % 2], z_in[d - 1, k % 2], (zi + d) % z_count)
+        elif k < 4:
+            @pl.when(jnp.logical_not(inner_plane))
+            def _():
+                z_put(k, zin.at[3 + k // 2, k % 2], z_mid[k], pair_z)
+        elif k < 6:
+            z_put(k, zin.at[1, k % 2], z_in[1, k % 2], pair_z)
+
+    def z_combine(k):
+        held = zin.at[3 + k // 2, k % 2]
+
+        @pl.when(inner_plane)
+        def _():
+            with jax.named_scope(f'w_mid#{k}'):
+                landing(held, z_mid[k]).wait_recv()
+            h, side = order[k // 2], k % 2
+            part[h, side, mine, :] = (
+                part[h, side, mine, :].astype(jnp.float32) + held[...].astype(jnp.float32)).astype(jnp.bfloat16)
+            z_put(k, zin.at[0, k % 2], z_in[0, k % 2], order[k // 2])
 
     far = z_count > KV_HEADS
+    squares = {}
+
+    def own_sum(side):
+        for n in sources:
+            with jax.named_scope(f'w_z#{n}'):
+                landing(zin.at[n, side], z_in[n, side]).wait_recv()
+        g = part[head, side, mine, :].astype(jnp.float32)
+        if not far:
+            g = g + sums[head, side, pl.ds(starts[last], final), :].astype(jnp.float32)
+        for n in sources:
+            g = g + zin[n, side].astype(jnp.float32)
+        cut = slice(side * HEAD, (side + 1) * HEAD)
+        grad[:, cut] = g
+        grad_b[:, cut] = g.astype(jnp.bfloat16)
+        squares[side] = jnp.sum(g * g, axis=0, keepdims=True)
+
     for t in range(chunks + last):
+        for k in range(4 if paired else 0):
+            if t == last + (3, 4, 5, 5)[k]:
+                z_combine(k)
         for i in range(dims):
             k = t - i
             if k < 0 or k >= chunks:
@@ -400,38 +463,21 @@
             with jax.named_scope(f'w_in#i={i}#k={k}'):
                 halves(i, k).wait_recv()
             if i == last and k // 2 == KV_HEADS - 1 and not far:
-                side = k % 2
-                grad[:, side * HEAD:(side + 1) * HEAD] = (
-                    part[head, side, mine, :].astype(jnp.float32)
-                    + sums[head, side, pl.ds(starts[last], final), :].astype(jnp.float32))
+                own_sum(k % 2)
                 continue
             add_in(i, k)
             if i < last:
                 pass_on(i + 1, k)
             else:
                 z_send(k)
+        if both == 2 and t == 5 and z_count > 2:
+            send_masters(1, [2])
         if t == 5:
             forward_block(0, False)
-            forward_block(1, both == 2)
-        if t == chunks - 2 and both == 2 and z_count > 2:
-            send_masters(1, [2])
     if far:
         for side in range(2):
-            grad[:, side * HEAD:(side + 1) * HEAD] = part[head, side, mine, :].astype(jnp.float32)
-
-    arrivals = [d for turn in turns for d in range(1, z_count) if d % KV_HEADS == turn]
-    own_square = jnp.zeros((1, HEAD), jnp.float32)
-    for d in arrivals:
-        for side in range(2):
-            with jax.named_scope(f'w_z#{d}'):
-                z_copy(d, side).wait_recv()
-            cut = slice(side * HEAD, (side + 1) * HEAD)
-            g = grad[:, cut] + zin[d - 1, side].astype(jnp.float32)
-            grad[:, cut] = g
-            if d == arrivals[-1]:
-                own_square = own_square + jnp.sum(g * g, axis=0, keepdims=True)
-                grad_b[:, cut] = g.astype(jnp.bfloat16)
-
+            own_sum(side)
+    own_square = squares[0] + squares[1]
     own_square = jnp.broadcast_to(jnp.sum(own_square, axis=1, keepdims=True), (1, LANES))
     small[1, :, :LANES] = own_square
     all_squares = to_all(small.at[1, :, pl.ds(0, LANES)], square_in, 2)
@@ -472,9 +518,15 @@
     for e in range(2, z_count):
         spread_block(e)
     if both == 2:
-        for e in range(3, z_count):
-            master_in(1, e).wait_recv()
-            second_block(e, beside)
+        for e in range(1, z_count):
+            with jax.named_scope(f'w_m2#{e}'):
+                master_in(1, e).wait_recv()
+
+        @pl.when(core == 1)
+        def _():
+            for e in range(1, min(z_count, 3)):
+                second_block(e, beside)
+    forward_block(1, both == 2)
 
     @pl.when(home_z != zi)
     def _():
@@ -528,8 +580,13 @@
         @pl.when(other_z == zi)
         def _():
             rows_in[head] = relay_in[...]
-    if z_count > 2:
-        forward_block(2, both == 2)
+    for e in range(2, z_count):
+        forward_block(e, both == 2)
+    if both == 2:
+        @pl.when(core == 1)
+        def _():
+            for e in range(3, z_count):
+                second_block(e, beside)
     for i in reversed(range(last)):
         for u in range(parts):
             with jax.named_scope(f'w_ag#{i + 1}#{u}'):
@@ -557,12 +614,7 @@
             hand_over[h].start()
 
     blocks = roll_ref.at[pl.ds(1, layer_count - 1), pl.ds(0, z_count * sub), :]
-    for e in range(3, z_count):
-        forward_block(e, False)
     if both == 2:
-        for e in range(1, min(z_count, 3)):
-            with jax.named_scope(f'w_m2#{e}'):
-                master_in(1, e).wait_recv()
         with jax.named_scope('w_fwd'):
             whole(blocks, FORWARD).wait_recv()
         for z in near:
@@ -600,7 +652,7 @@
 
     @pl.when(is_home)
     def _():
-        whole(zin, BASE).wait_send()
+        whole(zin.at[pl.ds(0, z_count - 1)], BASE).wait_send()
 
     for leaves, copy in nm_copies:
         pl.when(leaves)(copy.wait_send)
@@ -616,7 +668,7 @@
     whole(all_pieces, PIECES).wait_send()
     whole(roll_ref.at[0, pl.ds(0, (n_rep - 1) * final), :], GATHER).wait_send()
     whole(part.at[:, :, pl.ds(0, half - final), :], HALVES).wait_send()
-    whole(zin, GRADS).wait_send()
+    whole(zin.at[pl.ds(0, z_count - 1)], GRADS).wait_send()
     stats.wait_send()
     all_squares.wait_send()
 
@@ -640,7 +692,7 @@
     vmem, hbm = pl.BlockSpec(memory_space=pltpu.VMEM), pl.BlockSpec(memory_space=pltpu.HBM)
     dims = n_rep.bit_length() - 1
     both = 2 if split == 4 else 1
-    landings = 7 + 4 + 2 + KV_HEADS + both * (z_count - 1) + z_count + 8 * dims + 2 * (z_count - 1) + KV_HEADS * (n_rep // z_count) + 2 * dims
+    landings = 7 + 4 + 2 + 4 + KV_HEADS + both * (z_count - 1) + z_count + 8 * dims + 2 * (z_count - 1) + KV_HEADS * (n_rep // z_count) + 2 * dims
     return pl.pallas_call(
         functools.partial(step_kernel, n_rep, n_shard, split, groups),
         out_shape=(pltpu.VMEM((rows, cols), f32), pltpu.VMEM((layer_count, features, WIDE), bf16)),
@@ -664,7 +716,7 @@
             pltpu.VMEM((2 * toks, WIDE), bf16),
             pltpu.VMEM((KV_HEADS, 2, half, HEAD), bf16),
             pltpu.VMEM((KV_HEADS, 2, half, HEAD), bf16),
-            pltpu.VMEM((z_count - 1, 2, final, HEAD), bf16),
+            pltpu.VMEM((z_count + 1, 2, final, HEAD), bf16),
             pltpu.VMEM((final, WIDE), f32),
             pltpu.VMEM((final, WIDE), bf16),
             pltpu.VMEM((final, WIDE), bf16),

time: 77.8 us -> 74.1 us (0.952)
  the two profiles are of different devices: /device:TPU:13 before, /device:TPU:0 now
where the time goes in v4:
time: 74.1 us; the launch traced here: 73.9 us
  Pallas kernels  69.6 us (94%)
  local copies, waits for them, and re-layouts  3.67 us (5%)
    pallas_call x1, Pallas kernels, per_device(): pl.pallas_call(functools.partial(step_kernel, n_rep, n_shard, split, grou...  69.6 us
    unnamed x2, local copies, waits for them, and re-layouts  3.67 us

profile of v4, /device:TPU:0, one launch (start us, length us, event | category | flops | bytes accessed | tf_op | source)
XLA Modules:
  0.0 73.9 jit_solution(748842309965096622)
XLA Ops:
  0.6 69.6 %step.1 = (f32[448,1024]{1,0:T(8,128)S(1)}, bf16[3,3584,256]{2,1,0:T(8,128)(2,1)S(1)}) custom-call(s32[1,4]{1,0:T(1,128)} %group_hbm.1, f32[1,4]{1,0:T(1,128)} %reward_hbm.1, s32[1,448]{1,0:T(1,128)} %args_0_.4, s32[1,448]{1,0:T(1,128)} %args_1_.4, f32[1,448]{1,0:T(1,128)} %args_2_.4, f32[1,448]{1,0:T(1,128)} %args_3_.4, f32[1,448]{1,0:T(1,128)} %args_4_.4, ...), custom_call_target="tpu_custom_call" | custom-call | tf_op jit(solution)/shard_map/step/pallas_call | solution.py:696
  70.3 1.2 %copy.14 = f32[448,1024]{1,0:T(8,128)} copy(f32[448,1024]{1,0:T(8,128)S(1)} %get-tuple-element.2) | data formatting | bytes 3670016
  71.5 2.4 %copy.15 = bf16[3,3584,256]{2,1,0:T(8,128)(2,1)} copy(bf16[3,3584,256]{2,1,0:T(8,128)(2,1)S(1)} %get-tuple-element.3) | data formatting | bytes 11010048

commit v5 on v4

--- a/solution.py
+++ b/solution.py
@@ -470,7 +470,7 @@
                 pass_on(i + 1, k)
             else:
                 z_send(k)
-        if both == 2 and t == 5 and z_count > 2:
+        if both == 2 and t == 6 and z_count > 2:
             send_masters(1, [2])
         if t == 5:
             forward_block(0, False)
@@ -545,7 +545,7 @@
         roll_ref[0, span(row_me + t * inner, inner), :] = (
             base_in[at, :].astype(jnp.float32) - scale * grad[at, :]).astype(jnp.bfloat16)
 
-    parts = 2 if final // 2 % SUB == 0 else 1
+    parts = 4 if final // 4 % SUB == 0 else 1
     size = final // parts
     level_in = [[numbered() for _ in range(parts)] for _ in range(dims)]
 
@@ -671,6 +671,20 @@
     whole(zin.at[pl.ds(0, z_count - 1)], GRADS).wait_send()
     stats.wait_send()
     all_squares.wait_send()
+
+
+def copy_kernel(nm_ref, roll_ref, nm_out, roll_out, sems):
+    layer_count, features, _ = roll_ref.shape
+    copies = [pltpu.make_async_copy(nm_ref, nm_out, sems.at[0])]
+    for l in range(layer_count):
+        for n in range(2):
+            cut = pl.ds(n * (features // 2), features // 2)
+            copies.append(pltpu.make_async_copy(
+                roll_ref.at[l, cut], roll_out.at[l, cut], sems.at[1 + 2 * l + n]))
+    for copy in copies:
+        copy.start()
+    for copy in copies:
+        copy.wait()
 
 
 def per_device(
@@ -692,8 +706,8 @@
     vmem, hbm = pl.BlockSpec(memory_space=pltpu.VMEM), pl.BlockSpec(memory_space=pltpu.HBM)
     dims = n_rep.bit_length() - 1
     both = 2 if split == 4 else 1
-    landings = 7 + 4 + 2 + 4 + KV_HEADS + both * (z_count - 1) + z_count + 8 * dims + 2 * (z_count - 1) + KV_HEADS * (n_rep // z_count) + 2 * dims
-    return pl.pallas_call(
+    landings = 7 + 4 + 2 + 4 + KV_HEADS + both * (z_count - 1) + z_count + 8 * dims + 2 * (z_count - 1) + KV_HEADS * (n_rep // z_count) + 4 * dims
+    results = pl.pallas_call(
         functools.partial(step_kernel, n_rep, n_shard, split, groups),
         out_shape=(pltpu.VMEM((rows, cols), f32), pltpu.VMEM((layer_count, features, WIDE), bf16)),
         in_specs=[hbm] * 10,
@@ -737,6 +751,15 @@
         name="step",
     )(*(pltpu.with_memory_space_constraint(value, pltpu.HBM) for value in (
         group_ids, rewards, seq_ids, response_mask, new_logp, old_logp, ref_logp, hidden, cotangent, master)))
+    return pl.pallas_call(
+        copy_kernel,
+        out_shape=tuple(jax.ShapeDtypeStruct(value.shape, value.dtype) for value in results),
+        in_specs=[vmem] * 2,
+        out_specs=(hbm, hbm),
+        scratch_shapes=[pltpu.SemaphoreType.DMA((8,))],
+        compiler_params=pltpu.CompilerParams(vmem_limit_bytes=2**20),
+        name="copy",
+    )(*(pltpu.with_memory_space_constraint(value, pltpu.VMEM) for value in results))
 
 
 def solution(mesh):

time: 74.1 us -> 72.9 us (0.984)
  local copies, waits for them, and re-layouts: 3.67 us -> 0 us
  Pallas kernels: 69.6 us -> 72.1 us
    unnamed x2 -> x0, local copies, waits for them, and re-layouts: 3.67 us -> none
    pallas_call x0 -> x1, Pallas kernels: none -> 3.06 us  [per_device(): pl.pallas_call(copy_kernel, out_shape=tuple((jax.ShapeDtypeStruct(value.s...]
where the time goes in v5:
time: 72.9 us; the launch traced here: 72.7 us
  Pallas kernels  72.1 us (99%)
    pallas_call x1, Pallas kernels, per_device(): pl.pallas_call(functools.partial(step_kernel, n_rep, n_shard, split, grou...  69 us
    pallas_call x1, Pallas kernels, per_device(): pl.pallas_call(copy_kernel, out_shape=tuple((jax.ShapeDtypeStruct(value.s...  3.06 us

profile of v5, /device:TPU:0, one launch (start us, length us, event | category | flops | bytes accessed | tf_op | source)
XLA Modules:
  0.0 72.7 jit_solution(13759122909316491641)
XLA Ops:
  0.6 69.0 %step.1 = (f32[448,1024]{1,0:T(8,128)S(1)}, bf16[3,3584,256]{2,1,0:T(8,128)(2,1)S(1)}) custom-call(s32[1,4]{1,0:T(1,128)} %group_hbm.1, f32[1,4]{1,0:T(1,128)} %reward_hbm.1, s32[1,448]{1,0:T(1,128)} %args_0_.4, s32[1,448]{1,0:T(1,128)} %args_1_.4, f32[1,448]{1,0:T(1,128)} %args_2_.4, f32[1,448]{1,0:T(1,128)} %args_3_.4, f32[1,448]{1,0:T(1,128)} %args_4_.4, ...), custom_call_target="tpu_custom_call" | custom-call | tf_op jit(solution)/shard_map/step/pallas_call | solution.py:710
  69.7 3.1 %copy.13 = (f32[448,1024]{1,0:T(8,128)}, bf16[3,3584,256]{2,1,0:T(8,128)(2,1)}) custom-call(f32[448,1024]{1,0:T(8,128)S(1)} %get-tuple-element.4.nm_ref, bf16[3,3584,256]{2,1,0:T(8,128)(2,1)S(1)} %get-tuple-element.5.roll_ref), custom_call_target="tpu_custom_call" | custom-call | tf_op jit(solution)/shard_map/copy/pallas_call | solution.py:754

commit v6 on v5

--- a/solution.py
+++ b/solution.py
@@ -453,6 +453,16 @@
         squares[side] = jnp.sum(g * g, axis=0, keepdims=True)
 
     for t in range(chunks + last):
+        if t == chunks + last - 1:
+            for e in range(2, z_count):
+                spread_block(e)
+            if both == 2:
+                master_in(1, 1).wait_recv()
+
+                @pl.when(core == 1)
+                def _():
+                    second_block(1, beside)
+            forward_block(1, both == 2)
         for k in range(4 if paired else 0):
             if t == last + (3, 4, 5, 5)[k]:
                 z_combine(k)
@@ -515,18 +525,15 @@
     def _():
         rows_in[head, span(home_piece * final, final), :] = grad_b[...]
 
-    for e in range(2, z_count):
-        spread_block(e)
     if both == 2:
-        for e in range(1, z_count):
+        for e in range(2, z_count):
             with jax.named_scope(f'w_m2#{e}'):
                 master_in(1, e).wait_recv()
 
         @pl.when(core == 1)
         def _():
-            for e in range(1, min(z_count, 3)):
+            for e in range(2, min(z_count, 3)):
                 second_block(e, beside)
-    forward_block(1, both == 2)
 
     @pl.when(home_z != zi)
     def _():
@@ -555,8 +562,8 @@
     def gather_in(i, u):
         return landing(roll_ref.at[0, pl.ds(0, size << (dims - 1 - i)), :], level_in[i][u])
 
-    def gather_out(i, u):
-        for at in have[:1 << (last - i)]:
+    def gather_out(i, u, early=False):
+        for at in have[:1] if early else have[int(i == 0 < last):1 << (last - i)]:
             here = layer0(*at, u)
             put(here, here, partners[i], GATHER, level_in[i][u])
 
@@ -570,6 +577,8 @@
         have = have + [across(*at, i) for at in have]
     for u in range(parts):
         gather_out(last, u)
+    for u in range(parts if last else 0):
+        gather_out(0, u, True)
     piece_out(have[0])
     if relayed:
         for u in range(2):
@@ -621,6 +630,34 @@
             for xx in (x, 1 - x):
                 got = block(z, xx, 1 - yi)
                 put(got, got, mate, TO_MATE, TO_MATE)
+    @pl.when(core != keeper)
+    @jax.named_scope('w_hand')
+    def _():
+        for copy in hand_over:
+            copy.wait_recv()
+
+    for h in range(KV_HEADS):
+        for side in range(2):
+            low = side * KV_HEADS * HEAD + h * HEAD
+            nm_ref[:, low:low + HEAD] = (
+                m0[:, low:low + HEAD] - scale * rows_in[h, :, side * HEAD:(side + 1) * HEAD].astype(jnp.float32))
+
+    @pl.when(is_home)
+    def _():
+        whole(zin.at[pl.ds(0, z_count - 1)], BASE).wait_send()
+
+    for leaves, copy in nm_copies:
+        pl.when(leaves)(copy.wait_send)
+    for copy in mate_copies:
+        copy.wait_send()
+    whole(roll_ref.at[pl.ds(1, layer_count - 1), pl.ds(0, (z_count - 1) * both * sub), :], MASTERS).wait_send()
+    whole(blocks, SPREAD).wait_send()
+    if relayed:
+        whole(relay_in, RELAY).wait_send()
+    whole(part.at[:, :, pl.ds(0, half - final), :], HALVES).wait_send()
+    whole(zin.at[pl.ds(0, z_count - 1)], GRADS).wait_send()
+    stats.wait_send()
+    all_squares.wait_send()
     with jax.named_scope('w_gathered'):
         for u in range(parts):
             gather_in(0, u).wait_recv()
@@ -628,18 +665,6 @@
                 here = layer0(*at, u)
                 put(here, here, mate, PIECES, PIECES)
 
-    @pl.when(core != keeper)
-    @jax.named_scope('w_hand')
-    def _():
-        for copy in hand_over:
-            copy.wait_recv()
-
-    for h in range(KV_HEADS):
-        for side in range(2):
-            low = side * KV_HEADS * HEAD + h * HEAD
-            nm_ref[:, low:low + HEAD] = (
-                m0[:, low:low + HEAD] - scale * rows_in[h, :, side * HEAD:(side + 1) * HEAD].astype(jnp.float32))
-
     all_blocks = roll_ref.at[pl.ds(1, layer_count - 1), pl.ds(0, z_count * split * sub), :]
     all_pieces = roll_ref.at[0, pl.ds(0, n_rep * final), :]
     with jax.named_scope('w_mate'):
@@ -650,27 +675,11 @@
     def _():
         whole(rows_in, HAND).wait_send()
 
-    @pl.when(is_home)
-    def _():
-        whole(zin.at[pl.ds(0, z_count - 1)], BASE).wait_send()
-
-    for leaves, copy in nm_copies:
-        pl.when(leaves)(copy.wait_send)
-    for copy in mate_copies:
-        copy.wait_send()
-    whole(roll_ref.at[pl.ds(1, layer_count - 1), pl.ds(0, (z_count - 1) * both * sub), :], MASTERS).wait_send()
-    whole(blocks, SPREAD).wait_send()
     if both == 2:
         whole(blocks, FORWARD).wait_send()
-    if relayed:
-        whole(relay_in, RELAY).wait_send()
     whole(all_blocks, TO_MATE).wait_send()
     whole(all_pieces, PIECES).wait_send()
     whole(roll_ref.at[0, pl.ds(0, (n_rep - 1) * final), :], GATHER).wait_send()
-    whole(part.at[:, :, pl.ds(0, half - final), :], HALVES).wait_send()
-    whole(zin.at[pl.ds(0, z_count - 1)], GRADS).wait_send()
-    stats.wait_send()
-    all_squares.wait_send()
 
 
 def copy_kernel(nm_ref, roll_ref, nm_out, roll_out, sems):

time: 72.9 us -> 72.4 us (level)
  no operation moved by 1% of the time
where the time goes in v6:
time: 72.4 us; the launch traced here: 72.2 us
  Pallas kernels  71.6 us (99%)
    pallas_call x1, Pallas kernels, per_device(): pl.pallas_call(functools.partial(step_kernel, n_rep, n_shard, split, grou...  68.5 us
    pallas_call x1, Pallas kernels, per_device(): pl.pallas_call(copy_kernel, out_shape=tuple((jax.ShapeDtypeStruct(value.s...  3.06 us

profile of v6, /device:TPU:0, one launch (start us, length us, event | category | flops | bytes accessed | tf_op | source)
XLA Modules:
  0.0 72.2 jit_solution(17411526008329123539)
XLA Ops:
  0.6 68.5 %step.1 = (f32[448,1024]{1,0:T(8,128)S(1)}, bf16[3,3584,256]{2,1,0:T(8,128)(2,1)S(1)}) custom-call(s32[1,4]{1,0:T(1,128)} %group_hbm.1, f32[1,4]{1,0:T(1,128)} %reward_hbm.1, s32[1,448]{1,0:T(1,128)} %args_0_.4, s32[1,448]{1,0:T(1,128)} %args_1_.4, f32[1,448]{1,0:T(1,128)} %args_2_.4, f32[1,448]{1,0:T(1,128)} %args_3_.4, f32[1,448]{1,0:T(1,128)} %args_4_.4, ...), custom_call_target="tpu_custom_call" | custom-call | tf_op jit(solution)/shard_map/step/pallas_call | solution.py:719
  69.2 3.1 %copy.13 = (f32[448,1024]{1,0:T(8,128)}, bf16[3,3584,256]{2,1,0:T(8,128)(2,1)}) custom-call(f32[448,1024]{1,0:T(8,128)S(1)} %get-tuple-element.4.nm_ref, bf16[3,3584,256]{2,1,0:T(8,128)(2,1)S(1)} %get-tuple-element.5.roll_ref), custom_call_target="tpu_custom_call" | custom-call | tf_op jit(solution)/shard_map/copy/pallas_call | solution.py:763
